TPU v7x, 128 devices: a whole 4x4x4 slice. The times are simulated.
128 devices in a mesh: row: 8 (over z, core), col: 16 (over x, y).
Axes of the slice: x: 4, y: 4, z: 4, core: 2. Of those that a mesh axis runs over, the one named last changes fastest.
Arguments:
- point_coords: float32 [4096, 3, 256], P(('row', 'col')), may hold values from 0 to 10
- fluid_force: float32 [4096, 3, 256], P(('row', 'col')), may hold values from -6 to 6
- tile_clusters: int32 [4096, 8], P(('row', 'col')), may hold values from 0 to 2047, as said below
- pu_level: int32 [4096, 8, 256], P(('row', 'col')), may hold values from 0 to 15
- node_coords: float32 [2048, 3, 512], P(('row', 'col')), may hold values from 0 to 10
- node_disp: float32 [2048, 3, 512], P(('row', 'col')), may hold values from -6 to 6
- inverse: float32 [2048, 512, 512], P(('row', 'col')), may hold values from -0.25 to 0.25
Outputs:
- point_disp: float32 [4096, 3, 256], P(('row', 'col'))
- node_force: float32 [2048, 3, 512], P(('row', 'col'))
Inputs may be any that keep to these rules, and one draw needn't show every extreme that they name: `tile_clusters`: cluster c lives with rows c of the cluster arrays; tile t's k-th entry names a cluster intersecting it, possibly more than once in a tile. Among the 256 entries of one device's tiles, at most 8 name clusters of any one device (clusters d * 16 to d * 16 + 15).
All inputs are finite; a program needn't handle non-finite values.
Results may differ from a plain program's by a relative error of at most 0.0003.
Values sent between devices are 32-bit elements; how exact they have to be, the bound alone decides.
A program may use at most 128 MiB of HBM per device.

v0:
```python
import jax
import jax.numpy as jnp
from jax import lax
from jax.sharding import PartitionSpec as P

CAP = 8


def kernel(points, node_rows):
    offset = points[..., :, :, None] - node_rows[..., :, None, :]
    scaled = jnp.sqrt(jnp.sum(offset * offset, axis=-3))
    return jnp.maximum(1.0 - scaled, 0.0) ** 4 * (4.0 * scaled + 1.0)


def on_device(point_coords, fluid_force, tile_clusters, pu_level, node_coords, node_disp, inverse):
    highest = lax.Precision.HIGHEST
    devices = lax.axis_size(("row", "col"))
    slot_total = devices * CAP
    tile_total, kslots = tile_clusters.shape
    pair_total = tile_total * kslots
    node_count = node_coords.shape[2]
    local_count = node_coords.shape[0]
    coeffs = jnp.einsum("cin,cnm->cim", node_disp, inverse, precision=highest)
    levels = pu_level.astype(jnp.float32) + 1.0
    weights = levels / jnp.sum(levels, axis=1, keepdims=True)
    cluster_ids = tile_clusters.reshape(-1)
    owner_dev = cluster_ids // local_count
    local_id = cluster_ids % local_count
    owner_hits = (owner_dev[:, None] == jnp.arange(devices, dtype=jnp.int32)[None, :]).astype(
        jnp.int32
    )
    earlier = jnp.cumsum(owner_hits, axis=0) - owner_hits
    slot_of = owner_dev * CAP + jnp.sum(earlier * owner_hits, axis=1)
    slot_hits = slot_of[:, None] == jnp.arange(slot_total, dtype=jnp.int32)[None, :]
    wanted = jnp.sum(jnp.where(slot_hits, local_id[:, None] + 1, 0), axis=0) - 1
    asked_ids = lax.all_to_all(
        wanted.reshape(devices, CAP), ("row", "col"), split_axis=0, concat_axis=0, tiled=True
    ).reshape(slot_total)
    cluster_table = jnp.concatenate((coeffs, node_coords), axis=1)
    replies = jnp.take(cluster_table, jnp.maximum(asked_ids, 0), axis=0).reshape(
        devices, CAP, 6, node_count
    )
    arrived = lax.all_to_all(
        replies, ("row", "col"), split_axis=0, concat_axis=0, tiled=True
    ).reshape(slot_total, 6, node_count)
    own_rows = jnp.take(arrived, slot_of, axis=0).reshape(tile_total, kslots, 6, node_count)

    def per_tile(bundle):
        cluster_rows, points, tile_force, weight = bundle
        kernel_vals = kernel(points[None], cluster_rows[:, 3:])
        values = jnp.einsum("kpn,kin->kip", kernel_vals, cluster_rows[:, :3], precision=highest)
        shown_disp = jnp.sum(weight[:, None, :] * values, axis=0)
        loads = weight[:, None, :] * tile_force[None]
        partial_value = jnp.einsum("kpn,kip->kin", kernel_vals, loads, precision=highest)
        return (shown_disp, partial_value)

    point_disp, partial_value = lax.map(per_tile, (own_rows, point_coords, fluid_force, weights))
    outgoing = (
        jnp.zeros((slot_total, 3, node_count), jnp.float32)
        .at[slot_of]
        .set(partial_value.reshape(pair_total, 3, node_count))
    )
    returned = lax.all_to_all(
        outgoing.reshape(devices, CAP, 3, node_count),
        ("row", "col"),
        split_axis=0,
        concat_axis=0,
        tiled=True,
    ).reshape(slot_total, 3, node_count)
    chosen = (asked_ids[:, None] == jnp.arange(local_count, dtype=jnp.int32)[None, :]).astype(
        jnp.float32
    )
    node_force = jnp.einsum("sc,sin->cin", chosen, returned, precision=highest)
    return (point_disp, node_force)


def solution(mesh):
    placed = (
        P(("row", "col"), None, None),
        P(("row", "col"), None, None),
        P(("row", "col"), None),
        P(("row", "col"), None, None),
        P(("row", "col"), None, None),
        P(("row", "col"), None, None),
        P(("row", "col"), None, None),
    )
    return jax.shard_map(
        on_device,
        mesh=mesh,
        in_specs=placed,
        out_specs=(P(("row", "col"), None, None), P(("row", "col"), None, None)),
        check_vma=False,
    )
```

profile of v0, /device:TPU:0, one launch (start us, length us, event | category | flops | bytes accessed | tf_op | source)
XLA Modules:
  0.0 851.2 jit_solution(5510288235404094368)
XLA Ops:
  3.1 11.2 %all-to-all-start = ((s32[128,1,8]{2,1,0:T(1,128)}), s32[128,1,8]{2,1,0:T(1,128)S(1)}, u32[]{:S(2)}, u32[]{:S(2)}) async-start(s32[128,1,8]{2,1,0:T(1,128)} %bitcast.9), calls=%async_computation | async-start | bytes 131072 | tf_op jit(solution)/shard_map/all_to_all | solution.py:36
  15.3 11.7 %fusion.31 = f32[16,3,512]{2,1,0:T(4,128)S(1)} fusion(f32[16,512,512]{2,1,0:T(8,128)} %param.15, f32[16,3,512]{2,0,1:T(8,128)} %param.14), kind=kOutput, calls=%fused_computation.51 | convolution fusion | flops 150994944 | bytes 16973824 | tf_op jit(solution)/shard_map/cin,cnm->cim/dot_general | solution.py:23
  27.5 13.7 %gather_fusion = f32[1024,6,512]{2,1,0:T(8,128)} fusion(f32[16,6,512]{2,1,0:T(8,128)S(1)} %pad_maximum_fusion, s32[1024]{0:T(1024)S(1)} %broadcast_clamp_fusion), kind=kCustom, calls=%fused_computation | custom fusion | bytes 25169920 | tf_op jit(solution)/shard_map/jit(_take)/gather | solution.py:40
  41.3 23.8 %copy_select_fusion = f32[128,8,6,512]{3,1,2,0:T(8,128)} fusion(f32[128,8,6,512]{3,2,1,0:T(8,128)} %bitcast.61, pred[128,8]{1,0:T(8,128)(4,1)S(1)} %copy.103), kind=kLoop, calls=%fused_computation.35 | loop fusion | flops 3145728 | bytes 25166848 | tf_op jit(solution)/shard_map/jit(_take)/select_n | solution.py:40
  65.1 10.2 %all-to-all-start.1 = ((f32[128,8,6,512]{3,1,2,0:T(8,128)}), f32[128,8,6,512]{3,1,2,0:T(8,128)}, u32[]{:S(2)}, u32[]{:S(2)}) async-start(f32[128,8,6,512]{3,1,2,0:T(8,128)} %copy_select_fusion), calls=%async_computation.1 | async-start | bytes 25165824 | tf_op jit(solution)/shard_map/all_to_all | solution.py:43
  77.1 164.2 %all-to-all-done.1 = f32[128,8,6,512]{3,1,2,0:T(8,128)} async-done(((f32[128,8,6,512]{3,1,2,0:T(8,128)}), f32[128,8,6,512]{3,1,2,0:T(8,128)}, u32[]{:S(2)}, u32[]{:S(2)}) %all-to-all-start.1) | async-done | bytes 12582944 | tf_op jit(solution)/shard_map/all_to_all | solution.py:43
  241.3 11.3 %copy.133 = f32[128,8,6,512]{3,1,0,2:T(8,128)} copy(f32[128,8,6,512]{3,1,2,0:T(8,128)} %all-to-all-done.1) | data formatting | bytes 25165824 | tf_op jit(solution)/shard_map/all_to_all | solution.py:43
  252.6 17.8 %copy.110 = f32[1024,6,512]{2,1,0:T(8,128)} copy(f32[1024,6,512]{2,0,1:T(8,128)} %bitcast.62) | data formatting | bytes 25165824 | tf_op jit(solution)/shard_map/reshape | solution.py:45
  270.4 8.5 %gather_fusion.1 = f32[256,6,512]{2,1,0:T(8,128)} fusion(f32[1024,6,512]{2,1,0:T(8,128)} %copy.110, s32[1024]{0:T(1024)S(1)} %pad_clamp_fusion), kind=kCustom, calls=%fused_computation.1 | custom fusion | bytes 6292480 | tf_op jit(solution)/shard_map/jit(_take)/gather | solution.py:46
  282.7 435.7 %while.12 = (s32[]{:T(128)}, f32[32,3,256]{2,0,1:T(8,128)}, f32[32,8,3,512]{3,2,1,0:T(4,128)S(1)}, f32[32,8,256]{2,1,0:T(8,128)S(1)}, f32[32,8,6,512]{3,2,1,0:T(...) while((s32[]{:T(128)}, f32[32,3,256]{2,0,1:T(8,128)}, ...), condition=%wide.region_8.9_spmd, body=%wide.region_5.8_spmd.sunk | while | flops 98583808 | bytes 13138033 | solution.py:57
  290.0 5.1 fusion.52
  303.6 5.1 fusion.52
  317.2 5.1 fusion.52
  330.8 5.1 fusion.52
  344.4 5.1 fusion.52
  358.1 5.1 fusion.52
  371.7 5.1 fusion.52
  385.3 5.1 fusion.52
  398.9 5.1 fusion.52
  722.7 26.7 %scatter_fusion = f32[1024,3,512]{2,1,0:T(4,128)} fusion(f32[1024,3,512]{2,1,0:T(4,128)} %broadcast_in_dim.70, s32[256]{0:T(256)S(1)} %bitcast.74, f32[256,3,512]{2,1,0:T(4,128)S(1)} %bitcast.65), kind=kCustom, calls=%fused_computation.2 | custom fusion | bytes 4719616 | tf_op jit(solution)/shard_map/scatter | solution.py:61
  749.4 9.2 %copy.113 = f32[128,8,3,512]{3,1,2,0:T(8,128)} copy(f32[128,8,3,512]{3,2,1,0:T(4,128)} %bitcast.63) | data formatting | bytes 12582912 | tf_op jit(solution)/shard_map/reshape | solution.py:64
  758.6 12.6 %all-to-all-start.2 = ((f32[128,8,3,512]{3,1,2,0:T(8,128)}), f32[128,8,3,512]{3,1,2,0:T(8,128)}, u32[]{:S(2)}, u32[]{:S(2)}) async-start(f32[128,8,3,512]{3,1,2,0:T(8,128)} %copy.113), calls=%async_computation.2 | async-start | bytes 12582912 | tf_op jit(solution)/shard_map/all_to_all | solution.py:63
  772.6 72.8 %all-to-all-done.2 = f32[128,8,3,512]{3,1,2,0:T(8,128)} async-done(((f32[128,8,3,512]{3,1,2,0:T(8,128)}), f32[128,8,3,512]{3,1,2,0:T(8,128)}, u32[]{:S(2)}, u32[]{:S(2)}) %all-to-all-start.2) | async-done | bytes 6291488 | tf_op jit(solution)/shard_map/all_to_all | solution.py:63
  845.4 5.5 fusion.23
  (386 shorter events, 403.2 us)
Async XLA Ops:
  3.1 24.0 %all-to-all-start = ((s32[128,1,8]{2,1,0:T(1,128)}), s32[128,1,8]{2,1,0:T(1,128)S(1)}, u32[]{:S(2)}, u32[]{:S(2)}) async-start(s32[128,1,8]{2,1,0:T(1,128)} %bitcast.9), calls=%async_computation | async-start | bytes 131072 | tf_op jit(solution)/shard_map/all_to_all | solution.py:36
  65.1 10.5 %copy-start = (s32[32,8,256]{2,1,0:T(8,128)S(1)}, s32[32,8,256]{2,1,0:T(8,128)}, u32[]{:S(2)}) copy-start(s32[32,8,256]{2,1,0:T(8,128)} %param.12) | copy-start | bytes 786436
  65.1 176.2 %all-to-all-start.1 = ((f32[128,8,6,512]{3,1,2,0:T(8,128)}), f32[128,8,6,512]{3,1,2,0:T(8,128)}, u32[]{:S(2)}, u32[]{:S(2)}) async-start(f32[128,8,6,512]{3,1,2,0:T(8,128)} %copy_select_fusion), calls=%async_computation.1 | async-start | bytes 25165824 | tf_op jit(solution)/shard_map/all_to_all | solution.py:43
  758.6 86.8 %all-to-all-start.2 = ((f32[128,8,3,512]{3,1,2,0:T(8,128)}), f32[128,8,3,512]{3,1,2,0:T(8,128)}, u32[]{:S(2)}, u32[]{:S(2)}) async-start(f32[128,8,3,512]{3,1,2,0:T(8,128)} %copy.113), calls=%async_computation.2 | async-start | bytes 12582912 | tf_op jit(solution)/shard_map/all_to_all | solution.py:63
where the time goes:
time: 863 us; the launch traced here: 851 us
  matrix products  306 us (35%)
  waiting for transfers between devices  237 us (27%)
  local copies, waits for them, and re-layouts  195 us (23%)
  other arithmetic  76.8 us (9%)
  starting transfers between devices  34 us (4%)
    all_to_all x1, waiting for transfers between devices, on_device(): lax.all_to_all(replies, ('row', 'col'), split_axis=0, concat_axis=0, tile...  164 us
    dot_general x32, matrix products, per_tile(): jnp.einsum('kpn,kin->kip', kernel_vals, cluster_rows[:, :3], precision=hi...  163 us
    dot_general x32, matrix products, per_tile(): jnp.einsum('kpn,kip->kin', kernel_vals, loads, precision=highest)  126 us
    all_to_all x1, waiting for transfers between devices, on_device(): lax.all_to_all(outgoing.reshape(devices, CAP, 3, node_count), ('row', 'co...  72.8 us
    reduce_sum x32, other arithmetic, kernel(): scaled = jnp.sqrt(jnp.sum(offset * offset, axis=-3))  46 us
    dynamic_update_slice x64, local copies, waits for them, and re-layouts, on_device(): lax.map(per_tile, (own_rows, point_coords, fluid_force, weights))  44.2 us
    squeeze x32, local copies, waits for them, and re-layouts, on_device(): lax.map(per_tile, (own_rows, point_coords, fluid_force, weights))  29.4 us
    scatter x1, local copies, waits for them, and re-layouts, on_device(): outgoing = jnp.zeros((slot_total, 3, node_count), jnp.float32).at[slot_of...  26.7 us
  transfers between devices with their start and end apart: 3, of which 2 were waited for; matrix products, arithmetic and copies ran while one was open for 2% of the time, Pallas kernels for 0%

commit v1 on v0

v1 whole, which is shorter than its diff:
```python
import jax
import jax.numpy as jnp
from jax import lax
from jax.experimental import pallas as pl
from jax.experimental.pallas import tpu as pltpu
from jax.sharding import PartitionSpec as P

MESH = pl.DeviceIdType.MESH

def mod4(v):
    return lax.rem(v + 4, 4)

def place():
    row, col = lax.axis_index("row"), lax.axis_index("col")
    return [col // 4, lax.rem(col, 4), row // 2], lax.rem(row, 2)

def device(xyz, core):
    return (xyz[2] * 2 + core, xyz[0] * 4 + xyz[1])

def moved(xyz, dim, by):
    out = list(xyz)
    out[dim] = mod4(out[dim] + by)
    return out

def greet(xyz, core):
    barrier = pltpu.get_barrier_semaphore()
    for dim in range(3):
        for by in (1, -1):
            pl.semaphore_signal(barrier, inc=1, device_id=device(moved(xyz, dim, by), core), device_id_type=MESH)
    pl.semaphore_signal(barrier, inc=1, device_id=device(xyz, 1 - core), device_id_type=MESH)
    pl.semaphore_wait(barrier, 7)

ORDERS = ((0, 1, 2), (1, 2, 0), (2, 0, 1))

def gather_body(own_ref, out_ref, recv, send, near, sib_send, local):
    xyz, core = place()
    greet(xyz, core)
    half = own_ref.shape[1] // 2
    pend = []

    def push(src, dst, to, to_core, rsem, ssem):
        c = pltpu.make_async_remote_copy(src_ref=src, dst_ref=dst, send_sem=ssem, recv_sem=rsem,
                                         device_id=device(to, to_core), device_id_type=MESH)
        c.start()
        pend.append(c)

    def arrive(dst, rsem):
        pltpu.make_async_remote_copy(src_ref=dst, dst_ref=dst, send_sem=rsem, recv_sem=rsem,
                                     device_id=device(xyz, 1 - core), device_id_type=MESH).wait_recv()

    class Part:
        pass
    parts = []
    for p, (a, b, c) in enumerate(ORDERS):
        s = Part()
        s.p, s.a, s.b, s.c = p, a, b, c
        s.ia, s.ib, s.ic = xyz[a], xyz[b], xyz[c]
        s.nsend = 0
        parts.append(s)

    def block(s, ja, jb, jc, sub=None):
        r = out_ref.at[s.p, jc, jb, ja, core]
        return r if sub is None else r.at[sub]

    def group(s, jb, jc, k=None):
        return out_ref.at[s.p, jc, jb, :, core if k is None else k]

    def nsem(s):
        s.nsend += 1
        return send.at[s.p, s.nsend - 1]

    lo, hi = pl.ds(0, half), pl.ds(half, half)
    rel = lambda i, r: mod4(i + r)
    copies = []
    for s in parts:
        own = own_ref.at[s.p]
        cp = pltpu.make_async_copy(own, block(s, s.ia, s.ib, s.ic), local.at[s.p])
        cp.start()
        copies.append(cp)
        for d, by in ((0, 1), (1, -1)):
            push(own, block(s, s.ia, s.ib, s.ic), moved(xyz, s.a, by), core, recv.at[s.p, d], nsem(s))
    for s in parts:
        own = own_ref.at[s.p]
        for d, by in ((0, 1), (1, -1)):
            push(own, block(s, s.ia, s.ib, s.ic), moved(xyz, s.b, by), core, recv.at[s.p, 4 + 4 * d + 0], nsem(s))

    def send_b(s, r):
        ja = rel(s.ia, r)
        for d, by in ((0, 1), (1, -1)):
            push(block(s, ja, s.ib, s.ic), block(s, ja, s.ib, s.ic), moved(xyz, s.b, by), core,
                 recv.at[s.p, 4 + 4 * d + r], nsem(s))

    for s in parts:
        ja = rel(s.ia, -1)
        arrive(block(s, ja, s.ib, s.ic), recv.at[s.p, 0])
        push(block(s, ja, s.ib, s.ic, lo), block(s, ja, s.ib, s.ic, lo), moved(xyz, s.a, 1), core, recv.at[s.p, 2], nsem(s))
        ja2 = rel(s.ia, 1)
        arrive(block(s, ja2, s.ib, s.ic), recv.at[s.p, 1])
        push(block(s, ja2, s.ib, s.ic, hi), block(s, ja2, s.ib, s.ic, hi), moved(xyz, s.a, -1), core, recv.at[s.p, 3], nsem(s))
        send_b(s, 3)
        send_b(s, 1)

    def sib(s, jb, jc, slot):
        push(group(s, jb, jc), group(s, jb, jc), xyz, 1 - core, near.at[s.p, slot], sib_send.at[s.p, slot])

    def send_c(s, r):
        jb = rel(s.ib, r)
        for d, by in ((0, 1), (1, -1)):
            push(group(s, jb, s.ic), group(s, jb, s.ic), moved(xyz, s.c, by), core,
                 recv.at[s.p, 16 + 4 * d + r], nsem(s))
        sib(s, jb, s.ic, r)

    for s, cp in zip(parts, copies):
        ja = rel(s.ia, 2)
        arrive(block(s, ja, s.ib, s.ic, lo), recv.at[s.p, 2])
        arrive(block(s, ja, s.ib, s.ic, hi), recv.at[s.p, 3])
        send_b(s, 2)
        cp.wait()
        send_c(s, 0)
    for s in parts:
        for r in (0, 3, 1, 2):
            ja = rel(s.ia, r)
            for d, by in ((0, 1), (1, -1)):
                jb = rel(s.ib, -by)
                arrive(block(s, ja, jb, s.ic), recv.at[s.p, 4 + 4 * d + r])
                if (d == 0) == (r in (0, 3)):
                    push(block(s, ja, jb, s.ic), block(s, ja, jb, s.ic), moved(xyz, s.b, by), core,
                         recv.at[s.p, 12 + r], nsem(s))
        send_c(s, 3)
        send_c(s, 1)
    for s in parts:
        jb = rel(s.ib, 2)
        for r in (0, 3, 1, 2):
            arrive(block(s, rel(s.ia, r), jb, s.ic), recv.at[s.p, 12 + r])
        send_c(s, 2)
    for r in (0, 3, 1, 2):
        for s in parts:
            jb = rel(s.ib, r)
            for d, by in ((0, 1), (1, -1)):
                jc = rel(s.ic, -by)
                arrive(group(s, jb, jc), recv.at[s.p, 16 + 4 * d + r])
                if (d == 0) == (r in (0, 3)):
                    push(group(s, jb, jc), group(s, jb, jc), moved(xyz, s.c, by), core, recv.at[s.p, 24 + r], nsem(s))
                sib(s, jb, jc, 4 + 4 * d + r)
    for r in (0, 3, 1, 2):
        for s in parts:
            jb, jc = rel(s.ib, r), rel(s.ic, 2)
            arrive(group(s, jb, jc), recv.at[s.p, 24 + r])
            sib(s, jb, jc, 12 + r)
    for s in parts:
        for r in range(4):
            for slot, jc in ((r, s.ic), (4 + r, rel(s.ic, -1)), (8 + r, rel(s.ic, 1)), (12 + r, rel(s.ic, 2))):
                arrive(group(s, rel(s.ib, r), jc, 1 - core), near.at[s.p, slot])
    for c in pend:
        c.wait_send()

def all_gather(own):
    parts, clusters, rows, lanes = own.shape
    return pl.pallas_call(
        gather_body,
        out_shape=jax.ShapeDtypeStruct((parts, 4, 4, 4, 2, clusters, rows, lanes), jnp.float32),
        in_specs=[pl.BlockSpec(memory_space=pltpu.VMEM)],
        out_specs=pl.BlockSpec(memory_space=pl.ANY),
        scratch_shapes=[
            pltpu.SemaphoreType.DMA((3, 28)),
            pltpu.SemaphoreType.DMA((3, 28)),
            pltpu.SemaphoreType.DMA((3, 16)),
            pltpu.SemaphoreType.DMA((3, 16)),
            pltpu.SemaphoreType.DMA((3,)),
        ],
        compiler_params=pltpu.CompilerParams(collective_id=0, has_side_effects=True),
        name="torus_gather",
    )(own)


FIRST = (2, 3, 1, 0)
UP, DOWN = (2, 1), (3, 0)

def scatter_body(part_ref, out_ref, held, other, in_c, in_b, far_a, in_a,
                 load, near, near_send, rc, sc, rb, sb, ra, sa):
    xyz, core = place()
    pend = []
    rel = lambda i, r: mod4(i + r)
    info = []
    for p, (a, b, c) in enumerate(ORDERS):
        info.append((p, a, b, c, xyz[a], xyz[b], xyz[c]))

    def push(src, dst, to, to_core, rsem, ssem):
        cp = pltpu.make_async_remote_copy(src_ref=src, dst_ref=dst, send_sem=ssem, recv_sem=rsem,
                                          device_id=device(to, to_core), device_id_type=MESH)
        cp.start()
        pend.append(cp)

    def arrive(dst, rsem):
        pltpu.make_async_remote_copy(src_ref=dst, dst_ref=dst, send_sem=rsem, recv_sem=rsem,
                                     device_id=device(xyz, 1 - core), device_id_type=MESH).wait_recv()

    loads = {}
    def fetch(r4):
        for r in FIRST:
            for p, a, b, c, ia, ib, ic in info:
                jc, jb = rel(ic, r4), rel(ib, r)
                cp = pltpu.make_async_copy(part_ref.at[p, jc, jb, :, core], held.at[p, jc, jb], load.at[p, r4 * 4 + r])
                cp.start()
                loads[p, r4, r] = cp
    def swap(r4):
        for r in FIRST:
            for p, a, b, c, ia, ib, ic in info:
                jc, jb = rel(ic, r4), rel(ib, r)
                push(part_ref.at[p, jc, jb, :, 1 - core], other.at[p, jc, jb], xyz, 1 - core,
                     near.at[p, r4 * 4 + r], near_send.at[p, r4 * 4 + r])
    fetch(2)
    greet(xyz, core)
    for r4 in (2, 1, 3, 0):
        swap(r4)
        if r4 != 2:
            fetch(r4)

    def ready(p, r4, r, jc, jb):
        loads[p, r4, r].wait()
        arrive(other.at[p, jc, jb], near.at[p, r4 * 4 + r])

    for r in FIRST:
        for p, a, b, c, ia, ib, ic in info:
            jc, jb = rel(ic, 2), rel(ib, r)
            ready(p, 2, r, jc, jb)
            held[p, jc, jb] = held[p, jc, jb] + other[p, jc, jb]
            push(held.at[p, jc, jb], in_c.at[p, r], moved(xyz, c, 1 if r in UP else -1), core, rc.at[p, r], sc.at[p, r])
    for up, r, far in ((True, 3, False), (False, 2, False), (True, 0, False), (False, 1, False),
                       (True, 2, True), (False, 3, True), (True, 1, True), (False, 0, True)):
        for p, a, b, c, ia, ib, ic in info:
            by = 1 if up else -1
            jc, jb = rel(ic, by), rel(ib, r)
            ready(p, 1 if up else 3, r, jc, jb)
            if far:
                arrive(in_c.at[p, r], rc.at[p, r])
                held[p, jc, jb] = held[p, jc, jb] + other[p, jc, jb] + in_c[p, r]
            else:
                held[p, jc, jb] = held[p, jc, jb] + other[p, jc, jb]
            slot = (4 if up else 8) + r
            push(held.at[p, jc, jb], in_c.at[p, slot], moved(xyz, c, by), core, rc.at[p, slot], sc.at[p, slot])
    def finish_c(r):
        for p, a, b, c, ia, ib, ic in info:
            jc, jb = ic, rel(ib, r)
            ready(p, 0, r, jc, jb)
            arrive(in_c.at[p, 4 + r], rc.at[p, 4 + r])
            arrive(in_c.at[p, 8 + r], rc.at[p, 8 + r])
            held[p, jc, jb] = held[p, jc, jb] + other[p, jc, jb] + (in_c[p, 4 + r] + in_c[p, 8 + r])
    def send_b(p, b, jc, jb, ja, slot, by):
        push(held.at[p, jc, jb, ja], in_b.at[p, slot], moved(xyz, b, by), core, rb.at[p, slot], sb.at[p, slot])
    finish_c(2)
    for q in FIRST:
        for p, a, b, c, ia, ib, ic in info:
            send_b(p, b, ic, rel(ib, 2), rel(ia, q), q, 1 if q in UP else -1)
    finish_c(3)
    finish_c(1)
    for q in (3, 0):
        for p, a, b, c, ia, ib, ic in info:
            send_b(p, b, ic, rel(ib, 1), rel(ia, q), 4 + q, 1)
    for q in (2, 1):
        for p, a, b, c, ia, ib, ic in info:
            send_b(p, b, ic, rel(ib, 3), rel(ia, q), 8 + q, -1)
    for up, q in ((True, 2), (False, 3), (True, 1), (False, 0)):
        for p, a, b, c, ia, ib, ic in info:
            by = 1 if up else -1
            jc, jb, ja = ic, rel(ib, by), rel(ia, q)
            arrive(in_b.at[p, q], rb.at[p, q])
            held[p, jc, jb, ja] = held[p, jc, jb, ja] + in_b[p, q]
            send_b(p, b, jc, jb, ja, (4 if up else 8) + q, by)
    finish_c(0)
    def finish_b(q):
        for p, a, b, c, ia, ib, ic in info:
            ja = rel(ia, q)
            arrive(in_b.at[p, 4 + q], rb.at[p, 4 + q])
            arrive(in_b.at[p, 8 + q], rb.at[p, 8 + q])
            held[p, ic, ib, ja] = held[p, ic, ib, ja] + (in_b[p, 4 + q] + in_b[p, 8 + q])
    finish_b(2)
    lo, hi = pl.ds(0, 8), pl.ds(8, 8)
    for p, a, b, c, ia, ib, ic in info:
        blk = held.at[p, ic, ib, rel(ia, 2)]
        push(blk.at[lo], far_a.at[p, 0], moved(xyz, a, 1), core, ra.at[p, 0], sa.at[p, 0])
        push(blk.at[hi], far_a.at[p, 1], moved(xyz, a, -1), core, ra.at[p, 1], sa.at[p, 1])
    finish_b(1)
    finish_b(3)
    for p, a, b, c, ia, ib, ic in info:
        ja = rel(ia, 1)
        arrive(far_a.at[p, 0], ra.at[p, 0])
        held[p, ic, ib, ja, 0:8] = held[p, ic, ib, ja, 0:8] + far_a[p, 0]
        push(held.at[p, ic, ib, ja], in_a.at[p, 0], moved(xyz, a, 1), core, ra.at[p, 2], sa.at[p, 2])
        ja = rel(ia, 3)
        arrive(far_a.at[p, 1], ra.at[p, 1])
        held[p, ic, ib, ja, 8:16] = held[p, ic, ib, ja, 8:16] + far_a[p, 1]
        push(held.at[p, ic, ib, ja], in_a.at[p, 1], moved(xyz, a, -1), core, ra.at[p, 3], sa.at[p, 3])
    finish_b(0)
    for p, a, b, c, ia, ib, ic in info:
        arrive(in_a.at[p, 0], ra.at[p, 2])
        arrive(in_a.at[p, 1], ra.at[p, 3])
        out_ref[p] = held[p, ic, ib, ia] + (in_a[p, 0] + in_a[p, 1])
    for cp in pend:
        cp.wait_send()

def reduce_scatter(part):
    clusters, nodes = part.shape[-2:]
    D = pltpu.SemaphoreType.DMA
    V = lambda *s: pltpu.VMEM(s + (clusters, nodes), jnp.float32)
    return pl.pallas_call(
        scatter_body,
        out_shape=jax.ShapeDtypeStruct((3, clusters, nodes), jnp.float32),
        in_specs=[pl.BlockSpec(memory_space=pl.ANY)],
        out_specs=pl.BlockSpec(memory_space=pltpu.VMEM),
        scratch_shapes=[V(3, 4, 4, 4), V(3, 4, 4, 4), V(3, 12, 4), V(3, 12),
                        pltpu.VMEM((3, 2, clusters // 2, nodes), jnp.float32), V(3, 2),
                        D((3, 16)), D((3, 16)), D((3, 16)), D((3, 12)), D((3, 12)), D((3, 12)), D((3, 12)),
                        D((3, 4)), D((3, 4))],
        compiler_params=pltpu.CompilerParams(collective_id=1, has_side_effects=True, vmem_limit_bytes=40 * 2**20),
        name="torus_scatter",
    )(part)

ROWS = 32
UNROLL = 2

def pieces(value):
    high = value.astype(jnp.bfloat16)
    rest = value - high.astype(jnp.float32)
    mid = rest.astype(jnp.bfloat16)
    low = (rest - mid.astype(jnp.float32)).astype(jnp.bfloat16)
    return high, mid, low


def coeff_body(disp_ref, coords_ref, inverse_ref, table_ref):
    c = pl.program_id(0)
    nodes = inverse_ref.shape[-1]
    left = jnp.concatenate([disp_ref[i, pl.ds(c, 1), :] for i in range(3)] + [jnp.zeros((5, nodes), jnp.float32)], axis=0)
    lh = left.astype(jnp.bfloat16)
    ll = (left - lh.astype(jnp.float32)).astype(jnp.bfloat16)
    both = jnp.concatenate([lh, ll], axis=0)
    whole = inverse_ref[0]
    ih = whole.astype(jnp.bfloat16)
    il = (whole - ih.astype(jnp.float32)).astype(jnp.bfloat16)
    top = jnp.dot(both, ih, preferred_element_type=jnp.float32)
    low = jnp.dot(both, il, preferred_element_type=jnp.float32)
    res = top[0:8] + (top[8:16] + low[0:8])
    for i in range(6):
        row = coords_ref[i, pl.ds(c, 1), :] if i < 3 else res[i - 3:i - 2]
        for q in range(4):
            table_ref[i // 2, c, pl.ds((i % 2) * 4 + q, 1), :] = row[:, q * 128:(q + 1) * 128]


def own_table(node_disp, node_coords, inverse):
    clusters, nodes = inverse.shape[0], inverse.shape[1]
    whole = pl.BlockSpec((3, clusters, nodes), lambda c: (0, 0, 0))
    return pl.pallas_call(
        coeff_body,
        grid=(clusters,),
        out_shape=jax.ShapeDtypeStruct((3, clusters, 8, 128), jnp.float32),
        in_specs=[whole, whole, pl.BlockSpec((1, nodes, nodes), lambda c: (c, 0, 0))],
        out_specs=pl.BlockSpec((3, clusters, 8, 128), lambda c: (0, 0, 0, 0)),
        name="coefficients",
    )(node_disp, node_coords, inverse)


def pairs_body(ids_ref, pts_ref, frc_ref, lev_ref, table_ref, disp_ref, part_ref,
               rows, spots, raw, packed, mark, tally, flat, jobs, count, sem, sem2):
    tiles, slots = ids_ref.shape
    points = pts_ref.shape[-1]
    total = tiles * slots

    def start(q, carry):
        cid = ids_ref[q // slots, q % slots]
        l, dev = cid & 15, cid >> 4
        core, z = (dev >> 4) & 1, dev >> 5
        y, x = dev & 3, (dev >> 2) & 3
        for p, (a, b, c) in enumerate(((x, y, z), (y, z, x), (z, x, y))):
            f = (((c * 4 + b) * 4 + a) * 2 + core) * 16 + l
            flat[p, q] = f
            pltpu.make_async_copy(table_ref.at[p, pl.ds(pl.multiple_of(f * 8, 8), 8), :],
                                  rows.at[p, pl.ds(pl.multiple_of(q * 8, 8), 8), :], sem.at[p]).start()
        return carry
    lax.fori_loop(0, total, start, 0)

    def clear(g, carry):
        part_ref[0, pl.ds(pl.multiple_of(g * 16, 16), 16), :] = jnp.zeros((16, part_ref.shape[2]), jnp.float32)
        part_ref[1, pl.ds(pl.multiple_of(g * 16, 16), 16), :] = jnp.zeros((16, part_ref.shape[2]), jnp.float32)
        part_ref[2, pl.ds(pl.multiple_of(g * 16, 16), 16), :] = jnp.zeros((16, part_ref.shape[2]), jnp.float32)
        return carry
    lax.fori_loop(0, part_ref.shape[1] // 16, clear, 0)
    disp_ref[...] = jnp.zeros(disp_ref.shape, jnp.float32)

    def columns(t, carry):
        level = lev_ref[t].astype(jnp.float32) + 1.0
        weight = level / jnp.sum(level, axis=0, keepdims=True)
        raw[t, 6:14, :] = weight
        raw[t, 14:16, :] = jnp.zeros((2, points), jnp.float32)
        for i in range(3):
            raw[t, i:i + 1, :] = pts_ref[i, pl.ds(t, 1), :]
            raw[t, 3 + i:4 + i, :] = frc_ref[i, pl.ds(t, 1), :]
        h, m, l = pieces(raw[t])
        packed[t, 0:16, :] = h
        packed[t, 16:32, :] = m
        packed[t, 32:48, :] = l
        return carry
    lax.fori_loop(0, tiles, columns, 0, unroll=2)

    for p in range(3):
        pltpu.make_async_copy(table_ref.at[p, pl.ds(0, total * 8), :], rows.at[p], sem.at[p]).wait()

    def near(t, carry):
        dist = None
        for i in range(3):
            base = t * slots * 8 + (4 if i == 1 else 0)
            chunk = [rows[i // 2, pl.ds(base + r, slots, stride=8), :] for r in range(4)]
            low = jnp.minimum(jnp.minimum(chunk[0], chunk[1]), jnp.minimum(chunk[2], chunk[3]))
            high = jnp.maximum(jnp.maximum(chunk[0], chunk[1]), jnp.maximum(chunk[2], chunk[3]))
            low = jnp.min(low, axis=1, keepdims=True)
            high = jnp.max(high, axis=1, keepdims=True)
            at = pts_ref[i, pl.ds(t, 1), :]
            gap = jnp.maximum(jnp.maximum(low - at, at - high), 0.0)
            dist = gap * gap if dist is None else dist + gap * gap
        mark[pl.ds(pl.multiple_of(t * slots, slots), slots), :] = jnp.where(dist < 1.0001, 1.0, 0.0)
        return carry
    lax.fori_loop(0, tiles, near, 0, unroll=2)

    before = (lax.broadcasted_iota(jnp.int32, (points, points), 0) < lax.broadcasted_iota(jnp.int32, (points, points), 1))
    before = jnp.where(before, 1.0, 0.0).astype(jnp.bfloat16)
    flags = mark[...]
    ones = jnp.ones((16, points), jnp.bfloat16)
    fb = flags.astype(jnp.bfloat16)
    rank = jnp.dot(fb, before, preferred_element_type=jnp.float32)
    spots[...] = jnp.where(flags > 0.5, rank, -1.0)
    sums = lax.dot_general(ones, fb, (((1,), (1,)), ((), ())), preferred_element_type=jnp.float32)
    tally[...] = sums[0:8].astype(jnp.int32)
    cp = pltpu.make_async_copy(tally, count, sem2)
    cp.start()
    cp.wait()

    def list_pair(q, m):
        n = (count[0, q] + (ROWS - 1)) // ROWS
        def put(j, m):
            jobs[m] = q * 16 + j
            return m + 1
        return lax.fori_loop(0, n, put, m)
    made = lax.fori_loop(0, total, list_pair, 0)
    for u in range(UNROLL - 1):
        jobs[made + u] = points // ROWS
    trips = (made + UNROLL - 1) // UNROLL

    place32 = lax.broadcasted_iota(jnp.int32, (ROWS, points), 0).astype(jnp.float32)
    lane16 = lax.broadcasted_iota(jnp.int32, (ROWS, 16), 1)
    lane = lax.broadcasted_iota(jnp.int32, (ROWS, 128), 1)

    def one(job):
        q, j = job >> 4, job & 15
        t, k = q // slots, q % slots
        pick = jnp.where(place32 + (j * ROWS).astype(jnp.float32) == spots[pl.ds(q, 1), :], 1.0, 0.0).astype(jnp.bfloat16)
        got = lax.dot_general(pick, packed[t], (((1,), (1,)), ((), ())), preferred_element_type=jnp.float32)
        got = got[:, 0:16] + (got[:, 16:32] + got[:, 32:48])
        px, py, pz, fx, fy, fz = [got[:, i:i + 1] for i in range(6)]
        weight = jnp.sum(jnp.where(lane16 == 6 + k, got, 0.0), axis=1, keepdims=True)
        shown = [None] * 3
        loads = [[], [], []]
        for g in range(4):
            base = q * 8 + g
            dx = px - rows[0, pl.ds(base, 1), :]
            dy = py - rows[0, pl.ds(base + 4, 1), :]
            dz = pz - rows[1, pl.ds(base, 1), :]
            d2 = jnp.maximum(dx * dx + dy * dy + dz * dz, 1e-30)
            u = jnp.maximum(1.0 - d2 * lax.rsqrt(d2), 0.0)
            u2 = u * u
            val = (u2 * u2) * (5.0 - 4.0 * u) * weight
            for i, (pp, off) in enumerate(((1, 4), (2, 0), (2, 4))):
                term = val * rows[pp, pl.ds(base + off, 1), :]
                shown[i] = term if shown[i] is None else shown[i] + term
            for i, f in enumerate((fx, fy, fz)):
                loads[i].append(jnp.sum(val * f, axis=0, keepdims=True))
        cols = [jnp.sum(s, axis=1, keepdims=True) for s in shown]
        d = jnp.where(lane == 0, cols[0], jnp.where(lane == 1, cols[1], jnp.where(lane == 2, cols[2], 0.0)))
        dt = jnp.transpose(d)[0:8]
        dh = dt.astype(jnp.bfloat16)
        dl = (dt - dh.astype(jnp.float32)).astype(jnp.bfloat16)
        back = jnp.dot(jnp.concatenate([dh, dl], axis=0), pick, preferred_element_type=jnp.float32)
        back = back[0:8] + back[8:16]
        return q, t, back, [jnp.concatenate(l, axis=1) for l in loads]

    def trip(n, carry):
        done = [one(jobs[n * UNROLL + u]) for u in range(UNROLL)]
        for q, t, back, loads in done:
            for i in range(3):
                disp_ref[i, pl.ds(t, 1), :] += back[i:i + 1]
                part_ref[i, pl.ds(flat[i, q], 1), :] += loads[i]
        return carry
    lax.fori_loop(0, trips, trip, 0)


def pairs(ids, pts, frc, lev, table):
    tiles, slots = ids.shape
    points = pts.shape[-1]
    total = tiles * slots
    clusters = table.shape[1] // 8
    vm = pl.BlockSpec(memory_space=pltpu.VMEM)
    V = lambda s, d=jnp.float32: pltpu.VMEM(s, d)
    return pl.pallas_call(
        pairs_body,
        out_shape=(jax.ShapeDtypeStruct(pts.shape, jnp.float32), jax.ShapeDtypeStruct((3, clusters, 512), jnp.float32)),
        in_specs=[pl.BlockSpec(memory_space=pltpu.SMEM), vm, vm, vm, pl.BlockSpec(memory_space=pl.ANY)],
        out_specs=(vm, vm),
        scratch_shapes=[
            V((3, total * 8, 128)), V((total, points)), V((tiles, 16, points)), V((tiles, 48, points), jnp.bfloat16),
            V((total, points)), V((8, total), jnp.int32),
            pltpu.SMEM((3, total), jnp.int32), pltpu.SMEM((total * 8 + 8,), jnp.int32), pltpu.SMEM((8, total), jnp.int32),
            pltpu.SemaphoreType.DMA((3,)), pltpu.SemaphoreType.DMA,
        ],
        compiler_params=pltpu.CompilerParams(vmem_limit_bytes=40 * 2**20),
        name="pairs",
    )(ids, pts, frc, lev, table)


def on_device(point_coords, fluid_force, tile_clusters, pu_level, node_coords, node_disp, inverse):
    turn = lambda v: jnp.transpose(v, (1, 0, 2))
    table = all_gather(own_table(turn(node_disp), turn(node_coords), inverse))
    table = table.reshape(3, -1, 128)
    shown, part = pairs(tile_clusters, turn(point_coords), turn(fluid_force), pu_level, table)
    force = reduce_scatter(part.reshape(3, 4, 4, 4, 2, node_coords.shape[0], node_coords.shape[2]))
    return turn(shown), turn(force)


def solution(mesh):
    spec = P(("row", "col"), None, None)
    return jax.shard_map(
        on_device,
        mesh=mesh,
        in_specs=(spec, spec, P(("row", "col"), None), spec, spec, spec, spec),
        out_specs=(spec, spec),
        check_vma=False,
    )
```

time: 863 us -> 416 us (0.48); the launches traced: 851 us -> 415 us
  Pallas kernels: 0 us -> 403 us
  matrix products: 306 us -> 0 us
  waiting for transfers between devices: 237 us -> 0 us
  local copies, waits for them, and re-layouts: 195 us -> 10.5 us
  other arithmetic: 76.8 us -> 0 us
  starting transfers between devices: 34 us -> 0 us
    pallas_call x0 -> x4, Pallas kernels: none -> 403 us  [the longest x1 266 us: pairs(): pl.pallas_call(pairs_body, out_shape=(jax.ShapeDtypeStruct(pts.shape, jnp...]
    dot_general x66 -> x0, matrix products: 306 us -> none  [the longest x32 163 us: per_tile(): jnp.einsum('kpn,kin->kip', kernel_vals, cluster_rows[:, :3], precision=hi...]
    all_to_all x3 -> x0, waiting for transfers between devices: 237 us -> none  [the longest x1 164 us: on_device(): lax.all_to_all(replies, ('row', 'col'), split_axis=0, concat_axis=0, tile...]
    reduce_sum x34 -> x0, other arithmetic: 46.4 us -> none  [the longest x32 46 us: kernel(): scaled = jnp.sqrt(jnp.sum(offset * offset, axis=-3))]
    dynamic_update_slice x64 -> x0, local copies, waits for them, and re-layouts: 44.2 us -> none  [on_device(): lax.map(per_tile, (own_rows, point_coords, fluid_force, weights))]
    all_to_all x3 -> x0, starting transfers between devices: 34 us -> none  [the longest x1 12.6 us: on_device(): lax.all_to_all(outgoing.reshape(devices, CAP, 3, node_count), ('row', 'co...]
    squeeze x32 -> x0, local copies, waits for them, and re-layouts: 29.4 us -> none  [on_device(): lax.map(per_tile, (own_rows, point_coords, fluid_force, weights))]
    select_n x5 -> x0, other arithmetic: 27.7 us -> none  [the longest x1 23.8 us: on_device(): jnp.take(cluster_table, jnp.maximum(asked_ids, 0), axis=0)]
  transfers between devices with their start and end apart: 3 -> 0, of which waited for: 2 -> 0; matrix products, arithmetic and copies ran while one was open for 2% -> 0% of each run, Pallas kernels for 0% -> 0%
where the time goes in v1:
time: 416 us; the launch traced here: 415 us
  Pallas kernels  403 us (97%)
  local copies, waits for them, and re-layouts  10.5 us (3%)
    pallas_call x1, Pallas kernels, pairs(): pl.pallas_call(pairs_body, out_shape=(jax.ShapeDtypeStruct(pts.shape, jnp...  266 us
    pallas_call x1, Pallas kernels, all_gather(): pl.pallas_call(gather_body, out_shape=jax.ShapeDtypeStruct((parts, 4, 4,...  62.2 us
    pallas_call x1, Pallas kernels, reduce_scatter(): pl.pallas_call(scatter_body, out_shape=jax.ShapeDtypeStruct((3, clusters,...  62 us
    pallas_call x1, Pallas kernels, own_table(): pl.pallas_call(coeff_body, grid=(clusters,), out_shape=jax.ShapeDtypeStru...  13.5 us
    unnamed x12, local copies, waits for them, and re-layouts  10.5 us

profile of v1, /device:TPU:0, one launch (start us, length us, event | category | flops | bytes accessed | tf_op | source)
XLA Modules:
  0.0 414.6 jit_solution(10278410873526415660)
XLA Ops:
  0.6 0.8 copy.9.ids_ref
  1.4 13.5 %coefficients.1.own_ref = f32[3,16,8,128]{3,2,1,0:T(8,128)} custom-call(f32[3,16,512]{2,1,0:T(8,128)} %bitcast.13, f32[3,16,512]{2,1,0:T(8,128)} %bitcast.14, f32[16,512,512]{2,1,0:T(8,128)} %inverse_ref.1), custom_call_target="tpu_custom_call" | custom-call | tf_op jit(solution)/shard_map/coefficients/pallas_call | solution.py:352
  14.9 0.0 copy-start.2
  14.9 0.0 copy-start.3
  14.9 0.0 copy-start.4
  14.9 62.2 %torus_gather.1 = f32[3,4,4,4,2,16,8,128]{7,6,5,4,3,2,1,0:T(8,128)} custom-call(f32[3,16,8,128]{3,2,1,0:T(8,128)} %coefficients.1.own_ref), custom_call_target="tpu_custom_call" | custom-call | tf_op jit(solution)/shard_map/torus_gather/pallas_call | solution.py:159
  77.1 0.0 copy-done.2
  77.1 0.0 copy-done.3
  77.1 0.0 copy-done.4
  77.1 265.7 %pairs.1 = (f32[3,32,256]{2,1,0:T(8,128)}, f32[3,2048,512]{2,1,0:T(8,128)S(1)}) custom-call(s32[32,8]{1,0:T(8,128)S(1)} %copy.9.ids_ref, f32[3,32,256]{2,1,0:T(8,128)S(1)} %bitcast.10, f32[3,32,256]{2,1,0:T(8,128)S(1)} %bitcast.11, s32[32,8,256]{2,1,0:T(8,128)S(1)} %copy-done.2, f32[3,16384,128]{2,1,0:T(8,128)} %bitcast.12), custom_call_target="tpu_custom_call" | custom-call | tf_op jit(solution)/shard_map/pairs/pallas_call | solution.py:501
  342.9 0.0 copy-start
  342.9 4.5 %copy-done = f32[3,2048,512]{2,1,0:T(8,128)} copy-done((f32[3,2048,512]{2,1,0:T(8,128)}, f32[3,2048,512]{2,1,0:T(8,128)S(1)}, u32[]{:S(2)}) %copy-start) | copy-done | bytes 12582936
  347.4 0.0 copy-start.1
  347.4 4.6 %copy-done.1 = f32[3,2048,512]{2,1,0:T(8,128)S(1)} copy-done((f32[3,2048,512]{2,1,0:T(8,128)S(1)}, f32[3,2048,512]{2,1,0:T(8,128)}, u32[]{:S(2)}) %copy-start.1) | copy-done | bytes 12582936
  352.0 62.0 %torus_scatter.1 = f32[3,16,512]{2,1,0:T(8,128)S(1)} custom-call(f32[3,4,4,4,2,16,512]{6,5,4,3,2,1,0:T(8,128)S(1)} %bitcast.8), custom_call_target="tpu_custom_call" | custom-call | tf_op jit(solution)/shard_map/torus_scatter/pallas_call | solution.py:306
  413.9 0.6 copy.11
Async XLA Ops:
  14.9 62.2 %copy-start.2 = (s32[32,8,256]{2,1,0:T(8,128)S(1)}, s32[32,8,256]{2,1,0:T(8,128)}, u32[]{:S(2)}) copy-start(s32[32,8,256]{2,1,0:T(8,128)} %lev_ref.1) | copy-start | bytes 786436
  14.9 62.2 %copy-start.3 = (f32[32,3,256]{2,0,1:T(8,128)S(1)}, f32[32,3,256]{2,0,1:T(8,128)}, u32[]{:S(2)}) copy-start(f32[32,3,256]{2,0,1:T(8,128)} %param.7) | copy-start | bytes 294916
  14.9 62.2 %copy-start.4 = (f32[32,3,256]{2,0,1:T(8,128)S(1)}, f32[32,3,256]{2,0,1:T(8,128)}, u32[]{:S(2)}) copy-start(f32[32,3,256]{2,0,1:T(8,128)} %param.8) | copy-start | bytes 294916
  342.9 4.5 %copy-start = (f32[3,2048,512]{2,1,0:T(8,128)}, f32[3,2048,512]{2,1,0:T(8,128)S(1)}, u32[]{:S(2)}) copy-start(f32[3,2048,512]{2,1,0:T(8,128)S(1)} %get-tuple-element.5) | copy-start | bytes 37748740
  347.4 4.6 %copy-start.1 = (f32[3,2048,512]{2,1,0:T(8,128)S(1)}, f32[3,2048,512]{2,1,0:T(8,128)}, u32[]{:S(2)}) copy-start(f32[3,2048,512]{2,1,0:T(8,128)} %copy-done) | copy-start | bytes 37748740

commit v2 on v1

--- a/solution.py
+++ b/solution.py
@@ -160,7 +160,7 @@
         gather_body,
         out_shape=jax.ShapeDtypeStruct((parts, 4, 4, 4, 2, clusters, rows, lanes), jnp.float32),
         in_specs=[pl.BlockSpec(memory_space=pltpu.VMEM)],
-        out_specs=pl.BlockSpec(memory_space=pl.ANY),
+        out_specs=pl.BlockSpec(memory_space=pltpu.VMEM),
         scratch_shapes=[
             pltpu.SemaphoreType.DMA((3, 28)),
             pltpu.SemaphoreType.DMA((3, 28)),
@@ -168,7 +168,7 @@
             pltpu.SemaphoreType.DMA((3, 16)),
             pltpu.SemaphoreType.DMA((3,)),
         ],
-        compiler_params=pltpu.CompilerParams(collective_id=0, has_side_effects=True),
+        compiler_params=pltpu.CompilerParams(collective_id=0, has_side_effects=True, vmem_limit_bytes=2 * 2**20),
         name="torus_gather",
     )(own)
 
@@ -177,7 +177,7 @@
 UP, DOWN = (2, 1), (3, 0)
 
 def scatter_body(part_ref, out_ref, held, other, in_c, in_b, far_a, in_a,
-                 load, near, near_send, rc, sc, rb, sb, ra, sa):
+                 near, near_send, rc, sc, rb, sb, ra, sa):
     xyz, core = place()
     pend = []
     rel = lambda i, r: mod4(i + r)
@@ -195,36 +195,24 @@
         pltpu.make_async_remote_copy(src_ref=dst, dst_ref=dst, send_sem=rsem, recv_sem=rsem,
                                      device_id=device(xyz, 1 - core), device_id_type=MESH).wait_recv()
 
-    loads = {}
-    def fetch(r4):
-        for r in FIRST:
-            for p, a, b, c, ia, ib, ic in info:
-                jc, jb = rel(ic, r4), rel(ib, r)
-                cp = pltpu.make_async_copy(part_ref.at[p, jc, jb, :, core], held.at[p, jc, jb], load.at[p, r4 * 4 + r])
-                cp.start()
-                loads[p, r4, r] = cp
     def swap(r4):
         for r in FIRST:
             for p, a, b, c, ia, ib, ic in info:
                 jc, jb = rel(ic, r4), rel(ib, r)
                 push(part_ref.at[p, jc, jb, :, 1 - core], other.at[p, jc, jb], xyz, 1 - core,
                      near.at[p, r4 * 4 + r], near_send.at[p, r4 * 4 + r])
-    fetch(2)
     greet(xyz, core)
     for r4 in (2, 1, 3, 0):
         swap(r4)
-        if r4 != 2:
-            fetch(r4)
 
     def ready(p, r4, r, jc, jb):
-        loads[p, r4, r].wait()
         arrive(other.at[p, jc, jb], near.at[p, r4 * 4 + r])
 
     for r in FIRST:
         for p, a, b, c, ia, ib, ic in info:
             jc, jb = rel(ic, 2), rel(ib, r)
             ready(p, 2, r, jc, jb)
-            held[p, jc, jb] = held[p, jc, jb] + other[p, jc, jb]
+            held[p, jc, jb] = part_ref[p, jc, jb, :, core] + other[p, jc, jb]
             push(held.at[p, jc, jb], in_c.at[p, r], moved(xyz, c, 1 if r in UP else -1), core, rc.at[p, r], sc.at[p, r])
     for up, r, far in ((True, 3, False), (False, 2, False), (True, 0, False), (False, 1, False),
                        (True, 2, True), (False, 3, True), (True, 1, True), (False, 0, True)):
@@ -234,9 +222,9 @@
             ready(p, 1 if up else 3, r, jc, jb)
             if far:
                 arrive(in_c.at[p, r], rc.at[p, r])
-                held[p, jc, jb] = held[p, jc, jb] + other[p, jc, jb] + in_c[p, r]
+                held[p, jc, jb] = part_ref[p, jc, jb, :, core] + other[p, jc, jb] + in_c[p, r]
             else:
-                held[p, jc, jb] = held[p, jc, jb] + other[p, jc, jb]
+                held[p, jc, jb] = part_ref[p, jc, jb, :, core] + other[p, jc, jb]
             slot = (4 if up else 8) + r
             push(held.at[p, jc, jb], in_c.at[p, slot], moved(xyz, c, by), core, rc.at[p, slot], sc.at[p, slot])
     def finish_c(r):
@@ -245,7 +233,7 @@
             ready(p, 0, r, jc, jb)
             arrive(in_c.at[p, 4 + r], rc.at[p, 4 + r])
             arrive(in_c.at[p, 8 + r], rc.at[p, 8 + r])
-            held[p, jc, jb] = held[p, jc, jb] + other[p, jc, jb] + (in_c[p, 4 + r] + in_c[p, 8 + r])
+            held[p, jc, jb] = part_ref[p, jc, jb, :, core] + other[p, jc, jb] + (in_c[p, 4 + r] + in_c[p, 8 + r])
     def send_b(p, b, jc, jb, ja, slot, by):
         push(held.at[p, jc, jb, ja], in_b.at[p, slot], moved(xyz, b, by), core, rb.at[p, slot], sb.at[p, slot])
     finish_c(2)
@@ -306,17 +294,19 @@
     return pl.pallas_call(
         scatter_body,
         out_shape=jax.ShapeDtypeStruct((3, clusters, nodes), jnp.float32),
-        in_specs=[pl.BlockSpec(memory_space=pl.ANY)],
+        in_specs=[pl.BlockSpec(memory_space=pltpu.VMEM)],
         out_specs=pl.BlockSpec(memory_space=pltpu.VMEM),
         scratch_shapes=[V(3, 4, 4, 4), V(3, 4, 4, 4), V(3, 12, 4), V(3, 12),
                         pltpu.VMEM((3, 2, clusters // 2, nodes), jnp.float32), V(3, 2),
-                        D((3, 16)), D((3, 16)), D((3, 16)), D((3, 12)), D((3, 12)), D((3, 12)), D((3, 12)),
+                        D((3, 16)), D((3, 16)), D((3, 12)), D((3, 12)), D((3, 12)), D((3, 12)),
                         D((3, 4)), D((3, 4))],
-        compiler_params=pltpu.CompilerParams(collective_id=1, has_side_effects=True, vmem_limit_bytes=40 * 2**20),
+        compiler_params=pltpu.CompilerParams(collective_id=1, has_side_effects=True, vmem_limit_bytes=24 * 2**20),
         name="torus_scatter",
     )(part)
 
 ROWS = 32
+BATCH = 32
+WIDE = 32
 UNROLL = 2
 
 def pieces(value):
@@ -360,23 +350,23 @@
 
 
 def pairs_body(ids_ref, pts_ref, frc_ref, lev_ref, table_ref, disp_ref, part_ref,
-               rows, spots, raw, packed, mark, tally, flat, jobs, count, sem, sem2):
+               rows, spots, raw, packed, mark, picks, wide, moved_sum, spread_all, tally, flat, jobs, count, sem2):
     tiles, slots = ids_ref.shape
     points = pts_ref.shape[-1]
     total = tiles * slots
 
-    def start(q, carry):
-        cid = ids_ref[q // slots, q % slots]
-        l, dev = cid & 15, cid >> 4
-        core, z = (dev >> 4) & 1, dev >> 5
-        y, x = dev & 3, (dev >> 2) & 3
-        for p, (a, b, c) in enumerate(((x, y, z), (y, z, x), (z, x, y))):
-            f = (((c * 4 + b) * 4 + a) * 2 + core) * 16 + l
-            flat[p, q] = f
-            pltpu.make_async_copy(table_ref.at[p, pl.ds(pl.multiple_of(f * 8, 8), 8), :],
-                                  rows.at[p, pl.ds(pl.multiple_of(q * 8, 8), 8), :], sem.at[p]).start()
+    def fetch(t, carry):
+        for k in range(slots):
+            cid = ids_ref[t, k]
+            l, dev = cid & 15, cid >> 4
+            core, z = (dev >> 4) & 1, dev >> 5
+            y, x = dev & 3, (dev >> 2) & 3
+            for p, (a, b, c) in enumerate(((x, y, z), (y, z, x), (z, x, y))):
+                f = (((c * 4 + b) * 4 + a) * 2 + core) * 16 + l
+                flat[p, t * slots + k] = f
+                rows[p, pl.ds(pl.multiple_of((t * slots + k) * 8, 8), 8), :] = table_ref[p, pl.ds(pl.multiple_of(f * 8, 8), 8), :]
         return carry
-    lax.fori_loop(0, total, start, 0)
+    lax.fori_loop(0, tiles, fetch, 0)
 
     def clear(g, carry):
         part_ref[0, pl.ds(pl.multiple_of(g * 16, 16), 16), :] = jnp.zeros((16, part_ref.shape[2]), jnp.float32)
@@ -389,7 +379,7 @@
     def columns(t, carry):
         level = lev_ref[t].astype(jnp.float32) + 1.0
         weight = level / jnp.sum(level, axis=0, keepdims=True)
-        raw[t, 6:14, :] = weight
+        raw[t, 6:14, :] = weight * 4.0
         raw[t, 14:16, :] = jnp.zeros((2, points), jnp.float32)
         for i in range(3):
             raw[t, i:i + 1, :] = pts_ref[i, pl.ds(t, 1), :]
@@ -400,9 +390,6 @@
         packed[t, 32:48, :] = l
         return carry
     lax.fori_loop(0, tiles, columns, 0, unroll=2)
-
-    for p in range(3):
-        pltpu.make_async_copy(table_ref.at[p, pl.ds(0, total * 8), :], rows.at[p], sem.at[p]).wait()
 
     def near(t, carry):
         dist = None
@@ -433,29 +420,42 @@
     cp.start()
     cp.wait()
 
-    def list_pair(q, m):
-        n = (count[0, q] + (ROWS - 1)) // ROWS
-        def put(j, m):
-            jobs[m] = q * 16 + j
-            return m + 1
-        return lax.fori_loop(0, n, put, m)
-    made = lax.fori_loop(0, total, list_pair, 0)
-    for u in range(UNROLL - 1):
-        jobs[made + u] = points // ROWS
-    trips = (made + UNROLL - 1) // UNROLL
-
+    most = points // ROWS
+    def list_pairs(h, m):
+        for u in range(slots):
+            q = h * slots + u
+            for j in range(most):
+                jobs[m + j] = q * 16 + j
+            m = m + ((count[0, q] + (ROWS - 1)) >> 5)
+        return m
+    made = lax.fori_loop(0, tiles, list_pairs, 0)
+    for u in range(BATCH - 1):
+        jobs[made + u] = most
+    trips = (made + BATCH - 1) // BATCH
+
+    source = lax.broadcasted_iota(jnp.int32, (48, 6 * 128), 0) & 15
+    spread = jnp.where(source == (lax.broadcasted_iota(jnp.int32, (48, 6 * 128), 1) >> 7), 1.0, 0.0).astype(jnp.bfloat16)
+    spread_all[...] = spread
+    every = jnp.ones((48, 128), jnp.bfloat16)
+    lane48 = lax.broadcasted_iota(jnp.int32, (ROWS, 48), 1) & 15
     place32 = lax.broadcasted_iota(jnp.int32, (ROWS, points), 0).astype(jnp.float32)
-    lane16 = lax.broadcasted_iota(jnp.int32, (ROWS, 16), 1)
     lane = lax.broadcasted_iota(jnp.int32, (ROWS, 128), 1)
 
-    def one(job):
-        q, j = job >> 4, job & 15
+    def job_of(n):
+        job = jobs[n]
+        return job >> 4, job & 15
+
+    def bring(first, slot):
+        q, j = job_of(first + slot)
         t, k = q // slots, q % slots
         pick = jnp.where(place32 + (j * ROWS).astype(jnp.float32) == spots[pl.ds(q, 1), :], 1.0, 0.0).astype(jnp.bfloat16)
+        picks[slot] = pick
         got = lax.dot_general(pick, packed[t], (((1,), (1,)), ((), ())), preferred_element_type=jnp.float32)
-        got = got[:, 0:16] + (got[:, 16:32] + got[:, 32:48])
-        px, py, pz, fx, fy, fz = [got[:, i:i + 1] for i in range(6)]
-        weight = jnp.sum(jnp.where(lane16 == 6 + k, got, 0.0), axis=1, keepdims=True)
+        return got.astype(jnp.bfloat16), jnp.where(lane48 == 6 + k, got, 0.0).astype(jnp.bfloat16)
+
+    def work(first, slot):
+        q, j = job_of(first + slot)
+        px, py, pz, fx, fy, fz, weight = [wide[pl.ds(pl.multiple_of(slot * ROWS, ROWS), ROWS), i * 128:(i + 1) * 128] for i in range(7)]
         shown = [None] * 3
         loads = [[], [], []]
         for g in range(4):
@@ -466,27 +466,49 @@
             d2 = jnp.maximum(dx * dx + dy * dy + dz * dz, 1e-30)
             u = jnp.maximum(1.0 - d2 * lax.rsqrt(d2), 0.0)
             u2 = u * u
-            val = (u2 * u2) * (5.0 - 4.0 * u) * weight
+            val = ((u2 * u2) * weight) * (1.25 - u)
             for i, (pp, off) in enumerate(((1, 4), (2, 0), (2, 4))):
                 term = val * rows[pp, pl.ds(base + off, 1), :]
                 shown[i] = term if shown[i] is None else shown[i] + term
             for i, f in enumerate((fx, fy, fz)):
                 loads[i].append(jnp.sum(val * f, axis=0, keepdims=True))
-        cols = [jnp.sum(s, axis=1, keepdims=True) for s in shown]
-        d = jnp.where(lane == 0, cols[0], jnp.where(lane == 1, cols[1], jnp.where(lane == 2, cols[2], 0.0)))
+        for i in range(3):
+            moved_sum[slot, i] = shown[i]
+        return q, [jnp.concatenate(l, axis=1) for l in loads]
+
+    def give(first, slot):
+        q, j = job_of(first + slot)
+        cols = [jnp.sum(moved_sum[slot, i], axis=1, keepdims=True) for i in range(3)]
+        d = jnp.where(lane == 0, cols[0], jnp.where(lane == 1, cols[1], cols[2]))
         dt = jnp.transpose(d)[0:8]
         dh = dt.astype(jnp.bfloat16)
         dl = (dt - dh.astype(jnp.float32)).astype(jnp.bfloat16)
-        back = jnp.dot(jnp.concatenate([dh, dl], axis=0), pick, preferred_element_type=jnp.float32)
-        back = back[0:8] + back[8:16]
-        return q, t, back, [jnp.concatenate(l, axis=1) for l in loads]
+        back = jnp.dot(jnp.concatenate([dh, dl], axis=0), picks[slot], preferred_element_type=jnp.float32)
+        return q // slots, back[0:8] + back[8:16]
 
     def trip(n, carry):
-        done = [one(jobs[n * UNROLL + u]) for u in range(UNROLL)]
-        for q, t, back, loads in done:
-            for i in range(3):
-                disp_ref[i, pl.ds(t, 1), :] += back[i:i + 1]
-                part_ref[i, pl.ds(flat[i, q], 1), :] += loads[i]
+        first = n * BATCH
+        def do_bring(h, c):
+            took = [bring(first, h * WIDE + u) for u in range(WIDE)]
+            at = pl.ds(pl.multiple_of(h * (WIDE * ROWS), WIDE * ROWS), WIDE * ROWS)
+            got = jnp.concatenate([v[0] for v in took], axis=0)
+            wide[at, 0:6 * 128] = jnp.dot(got, spread_all[...], preferred_element_type=jnp.float32)
+            got = jnp.concatenate([v[1] for v in took], axis=0)
+            wide[at, 6 * 128:7 * 128] = jnp.dot(got, every, preferred_element_type=jnp.float32)
+            return c
+        lax.fori_loop(0, BATCH // WIDE, do_bring, 0)
+        def do_work(h, c):
+            for q, loads in [work(first, h * UNROLL + u) for u in range(UNROLL)]:
+                for i in range(3):
+                    part_ref[i, pl.ds(flat[i, q], 1), :] += loads[i]
+            return c
+        lax.fori_loop(0, BATCH // UNROLL, do_work, 0)
+        def do_give(h, c):
+            for t, back in [give(first, h * WIDE + u) for u in range(WIDE)]:
+                for i in range(3):
+                    disp_ref[i, pl.ds(t, 1), :] += back[i:i + 1]
+            return c
+        lax.fori_loop(0, BATCH // WIDE, do_give, 0)
         return carry
     lax.fori_loop(0, trips, trip, 0)
 
@@ -501,15 +523,17 @@
     return pl.pallas_call(
         pairs_body,
         out_shape=(jax.ShapeDtypeStruct(pts.shape, jnp.float32), jax.ShapeDtypeStruct((3, clusters, 512), jnp.float32)),
-        in_specs=[pl.BlockSpec(memory_space=pltpu.SMEM), vm, vm, vm, pl.BlockSpec(memory_space=pl.ANY)],
+        in_specs=[pl.BlockSpec(memory_space=pltpu.SMEM), vm, vm, vm, vm],
         out_specs=(vm, vm),
         scratch_shapes=[
             V((3, total * 8, 128)), V((total, points)), V((tiles, 16, points)), V((tiles, 48, points), jnp.bfloat16),
-            V((total, points)), V((8, total), jnp.int32),
-            pltpu.SMEM((3, total), jnp.int32), pltpu.SMEM((total * 8 + 8,), jnp.int32), pltpu.SMEM((8, total), jnp.int32),
-            pltpu.SemaphoreType.DMA((3,)), pltpu.SemaphoreType.DMA,
+            V((total, points)), V((BATCH, ROWS, points), jnp.bfloat16), V((BATCH * ROWS, 7 * 128)), V((BATCH, 3, ROWS, 128)),
+            V((48, 6 * 128), jnp.bfloat16),
+            V((8, total), jnp.int32),
+            pltpu.SMEM((3, total), jnp.int32), pltpu.SMEM((total * 8 + BATCH + 8,), jnp.int32), pltpu.SMEM((8, total), jnp.int32),
+            pltpu.SemaphoreType.DMA,
         ],
-        compiler_params=pltpu.CompilerParams(vmem_limit_bytes=40 * 2**20),
+        compiler_params=pltpu.CompilerParams(vmem_limit_bytes=16 * 2**20),
         name="pairs",
     )(ids, pts, frc, lev, table)
 

time: 416 us -> 192 us (0.46)
  Pallas kernels: 403 us -> 188 us
  local copies, waits for them, and re-layouts: 10.5 us -> 2.34 us
    pallas_call x1, Pallas kernels: 266 us -> 77.4 us  [pairs(): pl.pallas_call(pairs_body, out_shape=(jax.ShapeDtypeStruct(pts.shape, jnp...]
    pallas_call x1, Pallas kernels: 62 us -> 37 us  [reduce_scatter(): pl.pallas_call(scatter_body, out_shape=jax.ShapeDtypeStruct((3, clusters,...]
    unnamed x12 -> x10, local copies, waits for them, and re-layouts: 10.5 us -> 2.34 us
where the time goes in v2:
time: 192 us; the launch traced here: 191 us
  Pallas kernels  188 us (98%)
  local copies, waits for them, and re-layouts  2.34 us (1%)
    pallas_call x1, Pallas kernels, pairs(): pl.pallas_call(pairs_body, out_shape=(jax.ShapeDtypeStruct(pts.shape, jnp...  77.4 us
    pallas_call x1, Pallas kernels, all_gather(): pl.pallas_call(gather_body, out_shape=jax.ShapeDtypeStruct((parts, 4, 4,...  60.3 us
    pallas_call x1, Pallas kernels, reduce_scatter(): pl.pallas_call(scatter_body, out_shape=jax.ShapeDtypeStruct((3, clusters,...  37 us
    pallas_call x1, Pallas kernels, own_table(): pl.pallas_call(coeff_body, grid=(clusters,), out_shape=jax.ShapeDtypeStru...  13.5 us

profile of v2, /device:TPU:0, one launch (start us, length us, event | category | flops | bytes accessed | tf_op | source)
XLA Modules:
  0.0 191.3 jit_solution(15107609141343639915)
XLA Ops:
  0.6 0.8 copy.9.ids_ref
  1.4 13.5 %coefficients.1.own_ref = f32[3,16,8,128]{3,2,1,0:T(8,128)} custom-call(f32[3,16,512]{2,1,0:T(8,128)} %bitcast.13, f32[3,16,512]{2,1,0:T(8,128)} %bitcast.14, f32[16,512,512]{2,1,0:T(8,128)} %inverse_ref.1), custom_call_target="tpu_custom_call" | custom-call | tf_op jit(solution)/shard_map/coefficients/pallas_call | solution.py:342
  14.9 0.0 copy-start
  14.9 0.9 copy-done
  15.8 0.0 copy-start.1
  15.8 0.0 copy-start.2
  15.8 0.0 copy-start.3
  15.8 60.3 %torus_gather.1 = f32[3,4,4,4,2,16,8,128]{7,6,5,4,3,2,1,0:T(8,128)S(1)} custom-call(f32[3,16,8,128]{3,2,1,0:T(8,128)S(1)} %copy-done), custom_call_target="tpu_custom_call" | custom-call | tf_op jit(solution)/shard_map/torus_gather/pallas_call | solution.py:159
  76.1 0.0 copy-done.1
  76.2 0.0 copy-done.2
  76.2 0.0 copy-done.3
  76.2 77.4 %pairs.1 = (f32[3,32,256]{2,1,0:T(8,128)}, f32[3,2048,512]{2,1,0:T(8,128)S(1)}) custom-call(s32[32,8]{1,0:T(8,128)S(1)} %copy.9.ids_ref, f32[3,32,256]{2,1,0:T(8,128)S(1)} %bitcast.11, f32[3,32,256]{2,1,0:T(8,128)S(1)} %bitcast.12, s32[32,8,256]{2,1,0:T(8,128)S(1)} %copy-done.1, f32[3,16384,128]{2,1,0:T(8,128)S(1)} %bitcast.8), custom_call_target="tpu_custom_call" | custom-call | tf_op jit(solution)/shard_map/pairs/pallas_call | solution.py:523
  153.6 37.0 %torus_scatter.1 = f32[3,16,512]{2,1,0:T(8,128)S(1)} custom-call(f32[3,4,4,4,2,16,512]{6,5,4,3,2,1,0:T(8,128)S(1)} %bitcast.9), custom_call_target="tpu_custom_call" | custom-call | tf_op jit(solution)/shard_map/torus_scatter/pallas_call | solution.py:294
  190.6 0.6 copy.11
Async XLA Ops:
  14.9 0.9 copy-start
  15.8 60.4 %copy-start.1 = (s32[32,8,256]{2,1,0:T(8,128)S(1)}, s32[32,8,256]{2,1,0:T(8,128)}, u32[]{:S(2)}) copy-start(s32[32,8,256]{2,1,0:T(8,128)} %lev_ref.1) | copy-start | bytes 786436
  15.8 60.4 %copy-start.2 = (f32[32,3,256]{2,0,1:T(8,128)S(1)}, f32[32,3,256]{2,0,1:T(8,128)}, u32[]{:S(2)}) copy-start(f32[32,3,256]{2,0,1:T(8,128)} %param.7) | copy-start | bytes 294916
  15.8 60.4 %copy-start.3 = (f32[32,3,256]{2,0,1:T(8,128)S(1)}, f32[32,3,256]{2,0,1:T(8,128)}, u32[]{:S(2)}) copy-start(f32[32,3,256]{2,0,1:T(8,128)} %param.8) | copy-start | bytes 294916

commit v3 on v2

--- a/solution.py
+++ b/solution.py
@@ -305,9 +305,8 @@
     )(part)
 
 ROWS = 32
-BATCH = 32
-WIDE = 32
-UNROLL = 2
+GROUP = 2
+BATCH = 8
 
 def pieces(value):
     high = value.astype(jnp.bfloat16)
@@ -318,22 +317,23 @@
 
 
 def coeff_body(disp_ref, coords_ref, inverse_ref, table_ref):
-    c = pl.program_id(0)
     nodes = inverse_ref.shape[-1]
-    left = jnp.concatenate([disp_ref[i, pl.ds(c, 1), :] for i in range(3)] + [jnp.zeros((5, nodes), jnp.float32)], axis=0)
-    lh = left.astype(jnp.bfloat16)
-    ll = (left - lh.astype(jnp.float32)).astype(jnp.bfloat16)
-    both = jnp.concatenate([lh, ll], axis=0)
-    whole = inverse_ref[0]
-    ih = whole.astype(jnp.bfloat16)
-    il = (whole - ih.astype(jnp.float32)).astype(jnp.bfloat16)
-    top = jnp.dot(both, ih, preferred_element_type=jnp.float32)
-    low = jnp.dot(both, il, preferred_element_type=jnp.float32)
-    res = top[0:8] + (top[8:16] + low[0:8])
-    for i in range(6):
-        row = coords_ref[i, pl.ds(c, 1), :] if i < 3 else res[i - 3:i - 2]
-        for q in range(4):
-            table_ref[i // 2, c, pl.ds((i % 2) * 4 + q, 1), :] = row[:, q * 128:(q + 1) * 128]
+    for u in range(GROUP):
+        c = pl.program_id(0) * GROUP + u
+        left = jnp.concatenate([disp_ref[i, pl.ds(c, 1), :] for i in range(3)] + [jnp.zeros((5, nodes), jnp.float32)], axis=0)
+        lh = left.astype(jnp.bfloat16)
+        ll = (left - lh.astype(jnp.float32)).astype(jnp.bfloat16)
+        both = jnp.concatenate([lh, ll], axis=0)
+        whole = inverse_ref[u]
+        ih = whole.astype(jnp.bfloat16)
+        il = (whole - ih.astype(jnp.float32)).astype(jnp.bfloat16)
+        top = jnp.dot(both, ih, preferred_element_type=jnp.float32)
+        low = jnp.dot(both, il, preferred_element_type=jnp.float32)
+        res = top[0:8] + (top[8:16] + low[0:8])
+        for i in range(6):
+            row = coords_ref[i, pl.ds(c, 1), :] if i < 3 else res[i - 3:i - 2]
+            for q in range(4):
+                table_ref[i // 2, c, pl.ds((i % 2) * 4 + q, 1), :] = row[:, q * 128:(q + 1) * 128]
 
 
 def own_table(node_disp, node_coords, inverse):
@@ -341,16 +341,16 @@
     whole = pl.BlockSpec((3, clusters, nodes), lambda c: (0, 0, 0))
     return pl.pallas_call(
         coeff_body,
-        grid=(clusters,),
+        grid=(clusters // GROUP,),
         out_shape=jax.ShapeDtypeStruct((3, clusters, 8, 128), jnp.float32),
-        in_specs=[whole, whole, pl.BlockSpec((1, nodes, nodes), lambda c: (c, 0, 0))],
+        in_specs=[whole, whole, pl.BlockSpec((GROUP, nodes, nodes), lambda c: (c, 0, 0))],
         out_specs=pl.BlockSpec((3, clusters, 8, 128), lambda c: (0, 0, 0, 0)),
         name="coefficients",
     )(node_disp, node_coords, inverse)
 
 
 def pairs_body(ids_ref, pts_ref, frc_ref, lev_ref, table_ref, disp_ref, part_ref,
-               rows, spots, raw, packed, mark, picks, wide, moved_sum, spread_all, tally, flat, jobs, count, sem2):
+               rows, spots, raw, packed, mark, wide_a, wide_b, sums_a, sums_b, spread_all, tally, flat, jobs, count, sem2):
     tiles, slots = ids_ref.shape
     points = pts_ref.shape[-1]
     total = tiles * slots
@@ -428,10 +428,12 @@
                 jobs[m + j] = q * 16 + j
             m = m + ((count[0, q] + (ROWS - 1)) >> 5)
         return m
-    made = lax.fori_loop(0, tiles, list_pairs, 0)
-    for u in range(BATCH - 1):
+    for u in range(BATCH):
+        jobs[u] = most
+    made = lax.fori_loop(0, tiles, list_pairs, BATCH)
+    for u in range(4 * BATCH):
         jobs[made + u] = most
-    trips = (made + BATCH - 1) // BATCH
+    trips = (made - BATCH + 2 * BATCH - 1) // (2 * BATCH)
 
     source = lax.broadcasted_iota(jnp.int32, (48, 6 * 128), 0) & 15
     spread = jnp.where(source == (lax.broadcasted_iota(jnp.int32, (48, 6 * 128), 1) >> 7), 1.0, 0.0).astype(jnp.bfloat16)
@@ -441,76 +443,72 @@
     place32 = lax.broadcasted_iota(jnp.int32, (ROWS, points), 0).astype(jnp.float32)
     lane = lax.broadcasted_iota(jnp.int32, (ROWS, 128), 1)
 
-    def job_of(n):
-        job = jobs[n]
-        return job >> 4, job & 15
-
-    def bring(first, slot):
-        q, j = job_of(first + slot)
-        t, k = q // slots, q % slots
-        pick = jnp.where(place32 + (j * ROWS).astype(jnp.float32) == spots[pl.ds(q, 1), :], 1.0, 0.0).astype(jnp.bfloat16)
-        picks[slot] = pick
-        got = lax.dot_general(pick, packed[t], (((1,), (1,)), ((), ())), preferred_element_type=jnp.float32)
-        return got.astype(jnp.bfloat16), jnp.where(lane48 == 6 + k, got, 0.0).astype(jnp.bfloat16)
-
-    def work(first, slot):
-        q, j = job_of(first + slot)
-        px, py, pz, fx, fy, fz, weight = [wide[pl.ds(pl.multiple_of(slot * ROWS, ROWS), ROWS), i * 128:(i + 1) * 128] for i in range(7)]
-        shown = [None] * 3
-        loads = [[], [], []]
-        for g in range(4):
-            base = q * 8 + g
-            dx = px - rows[0, pl.ds(base, 1), :]
-            dy = py - rows[0, pl.ds(base + 4, 1), :]
-            dz = pz - rows[1, pl.ds(base, 1), :]
-            d2 = jnp.maximum(dx * dx + dy * dy + dz * dz, 1e-30)
-            u = jnp.maximum(1.0 - d2 * lax.rsqrt(d2), 0.0)
-            u2 = u * u
-            val = ((u2 * u2) * weight) * (1.25 - u)
-            for i, (pp, off) in enumerate(((1, 4), (2, 0), (2, 4))):
-                term = val * rows[pp, pl.ds(base + off, 1), :]
-                shown[i] = term if shown[i] is None else shown[i] + term
-            for i, f in enumerate((fx, fy, fz)):
-                loads[i].append(jnp.sum(val * f, axis=0, keepdims=True))
-        for i in range(3):
-            moved_sum[slot, i] = shown[i]
-        return q, [jnp.concatenate(l, axis=1) for l in loads]
-
-    def give(first, slot):
-        q, j = job_of(first + slot)
-        cols = [jnp.sum(moved_sum[slot, i], axis=1, keepdims=True) for i in range(3)]
-        d = jnp.where(lane == 0, cols[0], jnp.where(lane == 1, cols[1], cols[2]))
-        dt = jnp.transpose(d)[0:8]
-        dh = dt.astype(jnp.bfloat16)
-        dl = (dt - dh.astype(jnp.float32)).astype(jnp.bfloat16)
-        back = jnp.dot(jnp.concatenate([dh, dl], axis=0), picks[slot], preferred_element_type=jnp.float32)
-        return q // slots, back[0:8] + back[8:16]
+    def pick_of(job):
+        q, j = job >> 4, job & 15
+        return q, jnp.where(place32 + (j * ROWS).astype(jnp.float32) == spots[pl.ds(q, 1), :], 1.0, 0.0).astype(jnp.bfloat16)
+
+    def bring(batch, wide):
+        plain, chosen = [], []
+        for u in range(BATCH):
+            q, pick = pick_of(jobs[(batch + 1) * BATCH + u])
+            got = lax.dot_general(pick, packed[q // slots], (((1,), (1,)), ((), ())), preferred_element_type=jnp.float32)
+            plain.append(got.astype(jnp.bfloat16))
+            chosen.append(jnp.where(lane48 == 6 + q % slots, got, 0.0).astype(jnp.bfloat16))
+        wide[:, 0:6 * 128] = jnp.dot(jnp.concatenate(plain, axis=0), spread_all[...], preferred_element_type=jnp.float32)
+        wide[:, 6 * 128:7 * 128] = jnp.dot(jnp.concatenate(chosen, axis=0), every, preferred_element_type=jnp.float32)
+
+    def work(batch, wide, sums):
+        for slot in range(BATCH):
+            q = jobs[(batch + 1) * BATCH + slot] >> 4
+            px, py, pz, fx, fy, fz, weight = [wide[slot * ROWS:(slot + 1) * ROWS, i * 128:(i + 1) * 128] for i in range(7)]
+            shown = [None] * 3
+            loads = [[], [], []]
+            for g in range(4):
+                base = q * 8 + g
+                dx = px - rows[0, pl.ds(base, 1), :]
+                dy = py - rows[0, pl.ds(base + 4, 1), :]
+                dz = pz - rows[1, pl.ds(base, 1), :]
+                d2 = jnp.maximum(dx * dx + dy * dy + dz * dz, 1e-30)
+                u = jnp.maximum(1.0 - d2 * lax.rsqrt(d2), 0.0)
+                u2 = u * u
+                val = ((u2 * u2) * weight) * (1.25 - u)
+                for i, (pp, off) in enumerate(((1, 4), (2, 0), (2, 4))):
+                    term = val * rows[pp, pl.ds(base + off, 1), :]
+                    shown[i] = term if shown[i] is None else shown[i] + term
+                for i, f in enumerate((fx, fy, fz)):
+                    loads[i].append(jnp.sum(val * f, axis=0, keepdims=True))
+            for i in range(3):
+                sums[slot, i] = shown[i]
+                part_ref[i, pl.ds(flat[i, q], 1), :] += jnp.concatenate(loads[i], axis=1)
+
+    def give(batch, sums):
+        backs = []
+        for slot in range(BATCH):
+            q, pick = pick_of(jobs[(batch + 1) * BATCH + slot])
+            cols = [jnp.sum(sums[slot, i], axis=1, keepdims=True) for i in range(3)]
+            d = jnp.where(lane == 0, cols[0], jnp.where(lane == 1, cols[1], cols[2]))
+            dt = jnp.transpose(d)[0:8]
+            dh = dt.astype(jnp.bfloat16)
+            dl = (dt - dh.astype(jnp.float32)).astype(jnp.bfloat16)
+            back = jnp.dot(jnp.concatenate([dh, dl], axis=0), pick, preferred_element_type=jnp.float32)
+            backs.append((q // slots, back[0:8] + back[8:16]))
+        for t, back in backs:
+            for i in range(3):
+                disp_ref[i, pl.ds(t, 1), :] += back[i:i + 1]
+
+    sums_b[...] = jnp.zeros(sums_b.shape, jnp.float32)
+    bring(0, wide_a)
 
     def trip(n, carry):
-        first = n * BATCH
-        def do_bring(h, c):
-            took = [bring(first, h * WIDE + u) for u in range(WIDE)]
-            at = pl.ds(pl.multiple_of(h * (WIDE * ROWS), WIDE * ROWS), WIDE * ROWS)
-            got = jnp.concatenate([v[0] for v in took], axis=0)
-            wide[at, 0:6 * 128] = jnp.dot(got, spread_all[...], preferred_element_type=jnp.float32)
-            got = jnp.concatenate([v[1] for v in took], axis=0)
-            wide[at, 6 * 128:7 * 128] = jnp.dot(got, every, preferred_element_type=jnp.float32)
-            return c
-        lax.fori_loop(0, BATCH // WIDE, do_bring, 0)
-        def do_work(h, c):
-            for q, loads in [work(first, h * UNROLL + u) for u in range(UNROLL)]:
-                for i in range(3):
-                    part_ref[i, pl.ds(flat[i, q], 1), :] += loads[i]
-            return c
-        lax.fori_loop(0, BATCH // UNROLL, do_work, 0)
-        def do_give(h, c):
-            for t, back in [give(first, h * WIDE + u) for u in range(WIDE)]:
-                for i in range(3):
-                    disp_ref[i, pl.ds(t, 1), :] += back[i:i + 1]
-            return c
-        lax.fori_loop(0, BATCH // WIDE, do_give, 0)
+        bring(2 * n + 1, wide_b)
+        work(2 * n, wide_a, sums_a)
+        give(2 * n - 1, sums_b)
+        bring(2 * n + 2, wide_a)
+        work(2 * n + 1, wide_b, sums_b)
+        give(2 * n, sums_a)
         return carry
     lax.fori_loop(0, trips, trip, 0)
+    give(2 * trips - 1, sums_b)
 
 
 def pairs(ids, pts, frc, lev, table):
@@ -527,10 +525,11 @@
         out_specs=(vm, vm),
         scratch_shapes=[
             V((3, total * 8, 128)), V((total, points)), V((tiles, 16, points)), V((tiles, 48, points), jnp.bfloat16),
-            V((total, points)), V((BATCH, ROWS, points), jnp.bfloat16), V((BATCH * ROWS, 7 * 128)), V((BATCH, 3, ROWS, 128)),
+            V((total, points)), V((BATCH * ROWS, 7 * 128)), V((BATCH * ROWS, 7 * 128)),
+            V((BATCH, 3, ROWS, 128)), V((BATCH, 3, ROWS, 128)),
             V((48, 6 * 128), jnp.bfloat16),
             V((8, total), jnp.int32),
-            pltpu.SMEM((3, total), jnp.int32), pltpu.SMEM((total * 8 + BATCH + 8,), jnp.int32), pltpu.SMEM((8, total), jnp.int32),
+            pltpu.SMEM((3, total), jnp.int32), pltpu.SMEM((total * 8 + 5 * BATCH + 8,), jnp.int32), pltpu.SMEM((8, total), jnp.int32),
             pltpu.SemaphoreType.DMA,
         ],
         compiler_params=pltpu.CompilerParams(vmem_limit_bytes=16 * 2**20),

time: 192 us -> 169 us (0.88)
  Pallas kernels: 188 us -> 165 us
    pallas_call x1, Pallas kernels: 77.4 us -> 57.8 us  [pairs(): pl.pallas_call(pairs_body, out_shape=(jax.ShapeDtypeStruct(pts.shape, jnp...]
    pallas_call x1, Pallas kernels: 13.5 us -> 9.83 us  [own_table(): pl.pallas_call(coeff_body, grid=(clusters // GROUP,), out_shape=jax.Shape...]
where the time goes in v3:
time: 169 us; the launch traced here: 168 us
  Pallas kernels  165 us (98%)
  local copies, waits for them, and re-layouts  2.34 us (1%)
    pallas_call x1, Pallas kernels, all_gather(): pl.pallas_call(gather_body, out_shape=jax.ShapeDtypeStruct((parts, 4, 4,...  60.3 us
    pallas_call x1, Pallas kernels, pairs(): pl.pallas_call(pairs_body, out_shape=(jax.ShapeDtypeStruct(pts.shape, jnp...  57.8 us
    pallas_call x1, Pallas kernels, reduce_scatter(): pl.pallas_call(scatter_body, out_shape=jax.ShapeDtypeStruct((3, clusters,...  37.4 us
    pallas_call x1, Pallas kernels, own_table(): pl.pallas_call(coeff_body, grid=(clusters // GROUP,), out_shape=jax.Shape...  9.83 us

profile of v3, /device:TPU:0, one launch (start us, length us, event | category | flops | bytes accessed | tf_op | source)
XLA Modules:
  0.0 168.4 jit_solution(13978191059396493972)
XLA Ops:
  0.6 0.8 copy.9.ids_ref
  1.4 9.8 %coefficients.1.own_ref = f32[3,16,8,128]{3,2,1,0:T(8,128)} custom-call(f32[3,16,512]{2,1,0:T(8,128)} %bitcast.13, f32[3,16,512]{2,1,0:T(8,128)} %bitcast.14, f32[16,512,512]{2,1,0:T(8,128)} %inverse_ref.1), custom_call_target="tpu_custom_call" | custom-call | tf_op jit(solution)/shard_map/coefficients/pallas_call | solution.py:342
  11.2 0.0 copy-start
  11.2 0.9 copy-done
  12.1 0.0 copy-start.1
  12.2 0.0 copy-start.2
  12.2 0.0 copy-start.3
  12.2 60.3 %torus_gather.1 = f32[3,4,4,4,2,16,8,128]{7,6,5,4,3,2,1,0:T(8,128)S(1)} custom-call(f32[3,16,8,128]{3,2,1,0:T(8,128)S(1)} %copy-done), custom_call_target="tpu_custom_call" | custom-call | tf_op jit(solution)/shard_map/torus_gather/pallas_call | solution.py:159
  72.5 0.0 copy-done.1
  72.5 0.0 copy-done.2
  72.5 0.0 copy-done.3
  72.5 57.8 %pairs.1 = (f32[3,32,256]{2,1,0:T(8,128)}, f32[3,2048,512]{2,1,0:T(8,128)S(1)}) custom-call(s32[32,8]{1,0:T(8,128)S(1)} %copy.9.ids_ref, f32[3,32,256]{2,1,0:T(8,128)S(1)} %bitcast.11, f32[3,32,256]{2,1,0:T(8,128)S(1)} %bitcast.12, s32[32,8,256]{2,1,0:T(8,128)S(1)} %copy-done.1, f32[3,16384,128]{2,1,0:T(8,128)S(1)} %bitcast.8), custom_call_target="tpu_custom_call" | custom-call | tf_op jit(solution)/shard_map/pairs/pallas_call | solution.py:521
  130.4 37.4 %torus_scatter.1 = f32[3,16,512]{2,1,0:T(8,128)S(1)} custom-call(f32[3,4,4,4,2,16,512]{6,5,4,3,2,1,0:T(8,128)S(1)} %bitcast.9), custom_call_target="tpu_custom_call" | custom-call | tf_op jit(solution)/shard_map/torus_scatter/pallas_call | solution.py:294
  167.8 0.6 copy.11
Async XLA Ops:
  11.2 0.9 copy-start
  12.1 60.4 %copy-start.1 = (s32[32,8,256]{2,1,0:T(8,128)S(1)}, s32[32,8,256]{2,1,0:T(8,128)}, u32[]{:S(2)}) copy-start(s32[32,8,256]{2,1,0:T(8,128)} %lev_ref.1) | copy-start | bytes 786436
  12.2 60.4 %copy-start.2 = (f32[32,3,256]{2,0,1:T(8,128)S(1)}, f32[32,3,256]{2,0,1:T(8,128)}, u32[]{:S(2)}) copy-start(f32[32,3,256]{2,0,1:T(8,128)} %param.7) | copy-start | bytes 294916
  12.2 60.4 %copy-start.3 = (f32[32,3,256]{2,0,1:T(8,128)S(1)}, f32[32,3,256]{2,0,1:T(8,128)}, u32[]{:S(2)}) copy-start(f32[32,3,256]{2,0,1:T(8,128)} %param.8) | copy-start | bytes 294916

commit v4 on v3

--- a/solution.py
+++ b/solution.py
@@ -305,7 +305,7 @@
     )(part)
 
 ROWS = 32
-GROUP = 2
+GROUP = 4
 BATCH = 8
 
 def pieces(value):
@@ -344,27 +344,22 @@
         grid=(clusters // GROUP,),
         out_shape=jax.ShapeDtypeStruct((3, clusters, 8, 128), jnp.float32),
         in_specs=[whole, whole, pl.BlockSpec((GROUP, nodes, nodes), lambda c: (c, 0, 0))],
-        out_specs=pl.BlockSpec((3, clusters, 8, 128), lambda c: (0, 0, 0, 0)),
+        out_specs=pl.BlockSpec(memory_space=pltpu.VMEM),
+        compiler_params=pltpu.CompilerParams(vmem_limit_bytes=24 * 2**20),
         name="coefficients",
     )(node_disp, node_coords, inverse)
 
 
-def pairs_body(ids_ref, pts_ref, frc_ref, lev_ref, table_ref, disp_ref, part_ref,
-               rows, spots, raw, packed, mark, wide_a, wide_b, sums_a, sums_b, spread_all, tally, flat, jobs, count, sem2):
-    tiles, slots = ids_ref.shape
+def pairs_body(flat, pts_ref, frc_ref, lev_ref, table_ref, disp_ref, part_ref,
+               rows, spots, raw, packed, mark, wide_a, wide_b, sums_a, sums_b, spread_all, tally, jobs, count, sem2):
+    slots, tiles = flat.shape[1:]
     points = pts_ref.shape[-1]
     total = tiles * slots
 
     def fetch(t, carry):
         for k in range(slots):
-            cid = ids_ref[t, k]
-            l, dev = cid & 15, cid >> 4
-            core, z = (dev >> 4) & 1, dev >> 5
-            y, x = dev & 3, (dev >> 2) & 3
-            for p, (a, b, c) in enumerate(((x, y, z), (y, z, x), (z, x, y))):
-                f = (((c * 4 + b) * 4 + a) * 2 + core) * 16 + l
-                flat[p, t * slots + k] = f
-                rows[p, pl.ds(pl.multiple_of((t * slots + k) * 8, 8), 8), :] = table_ref[p, pl.ds(pl.multiple_of(f * 8, 8), 8), :]
+            for p in range(3):
+                rows[p, pl.ds(pl.multiple_of((t * slots + k) * 8, 8), 8), :] = table_ref[p, pl.ds(pl.multiple_of(flat[p, k, t] * 8, 8), 8), :]
         return carry
     lax.fori_loop(0, tiles, fetch, 0)
 
@@ -405,7 +400,7 @@
             dist = gap * gap if dist is None else dist + gap * gap
         mark[pl.ds(pl.multiple_of(t * slots, slots), slots), :] = jnp.where(dist < 1.0001, 1.0, 0.0)
         return carry
-    lax.fori_loop(0, tiles, near, 0, unroll=2)
+    lax.fori_loop(0, tiles, near, 0, unroll=4)
 
     before = (lax.broadcasted_iota(jnp.int32, (points, points), 0) < lax.broadcasted_iota(jnp.int32, (points, points), 1))
     before = jnp.where(before, 1.0, 0.0).astype(jnp.bfloat16)
@@ -479,7 +474,7 @@
                     loads[i].append(jnp.sum(val * f, axis=0, keepdims=True))
             for i in range(3):
                 sums[slot, i] = shown[i]
-                part_ref[i, pl.ds(flat[i, q], 1), :] += jnp.concatenate(loads[i], axis=1)
+                part_ref[i, pl.ds(flat[i, q & 7, q >> 3], 1), :] += jnp.concatenate(loads[i], axis=1)
 
     def give(batch, sums):
         backs = []
@@ -511,8 +506,8 @@
     give(2 * trips - 1, sums_b)
 
 
-def pairs(ids, pts, frc, lev, table):
-    tiles, slots = ids.shape
+def pairs(flat, pts, frc, lev, table):
+    slots, tiles = flat.shape[1:]
     points = pts.shape[-1]
     total = tiles * slots
     clusters = table.shape[1] // 8
@@ -529,19 +524,26 @@
             V((BATCH, 3, ROWS, 128)), V((BATCH, 3, ROWS, 128)),
             V((48, 6 * 128), jnp.bfloat16),
             V((8, total), jnp.int32),
-            pltpu.SMEM((3, total), jnp.int32), pltpu.SMEM((total * 8 + 5 * BATCH + 8,), jnp.int32), pltpu.SMEM((8, total), jnp.int32),
+            pltpu.SMEM((total * 8 + 5 * BATCH + 8,), jnp.int32), pltpu.SMEM((8, total), jnp.int32),
             pltpu.SemaphoreType.DMA,
         ],
         compiler_params=pltpu.CompilerParams(vmem_limit_bytes=16 * 2**20),
         name="pairs",
-    )(ids, pts, frc, lev, table)
+    )(flat, pts, frc, lev, table)
+
+
+def homes(ids):
+    l, dev = ids & 15, ids >> 4
+    core, z, y, x = (dev >> 4) & 1, dev >> 5, dev & 3, (dev >> 2) & 3
+    order = ((x, y, z), (y, z, x), (z, x, y))
+    return jnp.stack([(((c * 4 + b) * 4 + a) * 2 + core) * 16 + l for a, b, c in order])
 
 
 def on_device(point_coords, fluid_force, tile_clusters, pu_level, node_coords, node_disp, inverse):
     turn = lambda v: jnp.transpose(v, (1, 0, 2))
     table = all_gather(own_table(turn(node_disp), turn(node_coords), inverse))
     table = table.reshape(3, -1, 128)
-    shown, part = pairs(tile_clusters, turn(point_coords), turn(fluid_force), pu_level, table)
+    shown, part = pairs(homes(tile_clusters.T), turn(point_coords), turn(fluid_force), pu_level, table)
     force = reduce_scatter(part.reshape(3, 4, 4, 4, 2, node_coords.shape[0], node_coords.shape[2]))
     return turn(shown), turn(force)
 

time: 169 us -> 167 us (0.988)
  Pallas kernels: 165 us -> 156 us
  local copies, waits for them, and re-layouts: 2.34 us -> 8.24 us
    pallas_call x1, Pallas kernels: 9.83 us -> 2.84 us  [own_table(): pl.pallas_call(coeff_body, grid=(clusters // GROUP,), out_shape=jax.Shape...]
    unnamed x10 -> x13, local copies, waits for them, and re-layouts: 2.34 us -> 8.24 us
    pallas_call x1, Pallas kernels: 57.8 us -> 53.2 us  [pairs(): pl.pallas_call(pairs_body, out_shape=(jax.ShapeDtypeStruct(pts.shape, jnp...]
    pallas_call x1, Pallas kernels: 37.4 us -> 39.6 us  [reduce_scatter(): pl.pallas_call(scatter_body, out_shape=jax.ShapeDtypeStruct((3, clusters,...]
where the time goes in v4:
time: 167 us; the launch traced here: 166 us
  Pallas kernels  156 us (93%)
  local copies, waits for them, and re-layouts  8.24 us (5%)
    pallas_call x1, Pallas kernels, all_gather(): pl.pallas_call(gather_body, out_shape=jax.ShapeDtypeStruct((parts, 4, 4,...  60.4 us
    pallas_call x1, Pallas kernels, pairs(): pl.pallas_call(pairs_body, out_shape=(jax.ShapeDtypeStruct(pts.shape, jnp...  53.2 us
    pallas_call x1, Pallas kernels, reduce_scatter(): pl.pallas_call(scatter_body, out_shape=jax.ShapeDtypeStruct((3, clusters,...  39.6 us
    unnamed x13, local copies, waits for them, and re-layouts  8.24 us

profile of v4, /device:TPU:0, one launch (start us, length us, event | category | flops | bytes accessed | tf_op | source)
XLA Modules:
  0.0 165.8 jit_solution(6986040859742043681)
XLA Ops:
  0.6 0.7 fusion
  1.3 0.0 copy-start
  1.3 5.8 %copy-done = f32[16,512,512]{2,1,0:T(8,128)S(1)} copy-done((f32[16,512,512]{2,1,0:T(8,128)S(1)}, f32[16,512,512]{2,1,0:T(8,128)}, u32[]{:S(2)}) %copy-start) | copy-done | bytes 16777240
  7.1 0.0 copy-start.2
  7.1 0.9 copy-done.2
  8.0 0.0 copy-start.3
  8.0 0.9 copy-done.3
  8.9 2.8 %coefficients.1.own_ref = f32[3,16,8,128]{3,2,1,0:T(8,128)S(1)} custom-call(f32[3,16,512]{2,1,0:T(8,128)S(1)} %bitcast.85, f32[3,16,512]{2,1,0:T(8,128)S(1)} %bitcast.86, f32[16,512,512]{2,1,0:T(8,128)S(1)} %copy-done), custom_call_target="tpu_custom_call" | custom-call | tf_op jit(solution)/shard_map/coefficients/pallas_call | solution.py:342
  11.7 0.0 copy-start.1
  11.7 0.0 copy-start.4
  11.8 0.0 copy-start.5
  11.8 60.4 %torus_gather.1 = f32[3,4,4,4,2,16,8,128]{7,6,5,4,3,2,1,0:T(8,128)S(1)} custom-call(f32[3,16,8,128]{3,2,1,0:T(8,128)S(1)} %coefficients.1.own_ref), custom_call_target="tpu_custom_call" | custom-call | tf_op jit(solution)/shard_map/torus_gather/pallas_call | solution.py:159
  72.2 0.0 copy-done.1
  72.2 0.0 copy-done.4
  72.3 0.0 copy-done.5
  72.3 53.2 %pairs.1 = (f32[3,32,256]{2,1,0:T(8,128)}, f32[3,2048,512]{2,1,0:T(8,128)S(1)}) custom-call(s32[3,8,32]{2,1,0:T(8,128)S(1)} %pad_add_fusion.flat, f32[3,32,256]{2,1,0:T(8,128)S(1)} %bitcast.87, f32[3,32,256]{2,1,0:T(8,128)S(1)} %bitcast.88, s32[32,8,256]{2,1,0:T(8,128)S(1)} %copy-done.1, f32[3,16384,128]{2,1,0:T(8,128)S(1)} %bitcast.82), custom_call_target="tpu_custom_call" | custom-call | tf_op jit(solution)/shard_map/pairs/pallas_call | solution.py:516
  125.5 39.6 %torus_scatter.1 = f32[3,16,512]{2,1,0:T(8,128)S(1)} custom-call(f32[3,4,4,4,2,16,512]{6,5,4,3,2,1,0:T(8,128)S(1)} %bitcast.83), custom_call_target="tpu_custom_call" | custom-call | tf_op jit(solution)/shard_map/torus_scatter/pallas_call | solution.py:294
  165.2 0.6 copy.10
  (1 shorter events, 0.0 us)
Async XLA Ops:
  1.3 5.8 %copy-start = (f32[16,512,512]{2,1,0:T(8,128)S(1)}, f32[16,512,512]{2,1,0:T(8,128)}, u32[]{:S(2)}) copy-start(f32[16,512,512]{2,1,0:T(8,128)} %inverse_ref.1) | copy-start | bytes 50331652
  7.1 0.9 copy-start.2
  8.0 0.9 copy-start.3
  11.7 60.5 %copy-start.1 = (s32[32,8,256]{2,1,0:T(8,128)S(1)}, s32[32,8,256]{2,1,0:T(8,128)}, u32[]{:S(2)}) copy-start(s32[32,8,256]{2,1,0:T(8,128)} %lev_ref.1) | copy-start | bytes 786436
  11.7 60.5 %copy-start.4 = (f32[32,3,256]{2,0,1:T(8,128)S(1)}, f32[32,3,256]{2,0,1:T(8,128)}, u32[]{:S(2)}) copy-start(f32[32,3,256]{2,0,1:T(8,128)} %param.7) | copy-start | bytes 294916
  11.8 60.5 %copy-start.5 = (f32[32,3,256]{2,0,1:T(8,128)S(1)}, f32[32,3,256]{2,0,1:T(8,128)}, u32[]{:S(2)}) copy-start(f32[32,3,256]{2,0,1:T(8,128)} %param.8) | copy-start | bytes 294916

commit v5 on v4

--- a/solution.py
+++ b/solution.py
@@ -345,7 +345,7 @@
         out_shape=jax.ShapeDtypeStruct((3, clusters, 8, 128), jnp.float32),
         in_specs=[whole, whole, pl.BlockSpec((GROUP, nodes, nodes), lambda c: (c, 0, 0))],
         out_specs=pl.BlockSpec(memory_space=pltpu.VMEM),
-        compiler_params=pltpu.CompilerParams(vmem_limit_bytes=24 * 2**20),
+        compiler_params=pltpu.CompilerParams(vmem_limit_bytes=56 * 2**20),
         name="coefficients",
     )(node_disp, node_coords, inverse)
 

time: 167 us -> 164 us (0.982)
  local copies, waits for them, and re-layouts: 8.24 us -> 1.58 us
  Pallas kernels: 156 us -> 161 us
    unnamed x13 -> x9, local copies, waits for them, and re-layouts: 8.24 us -> 1.58 us
    pallas_call x1, Pallas kernels: 2.84 us -> 8.09 us  [own_table(): pl.pallas_call(coeff_body, grid=(clusters // GROUP,), out_shape=jax.Shape...]
    pallas_call x1, Pallas kernels: 39.6 us -> 37.4 us  [reduce_scatter(): pl.pallas_call(scatter_body, out_shape=jax.ShapeDtypeStruct((3, clusters,...]
    pallas_call x1, Pallas kernels: 53.2 us -> 54.9 us  [pairs(): pl.pallas_call(pairs_body, out_shape=(jax.ShapeDtypeStruct(pts.shape, jnp...]
where the time goes in v5:
time: 164 us
  Pallas kernels  161 us (98%)
    pallas_call x1, Pallas kernels, all_gather(): pl.pallas_call(gather_body, out_shape=jax.ShapeDtypeStruct((parts, 4, 4,...  60.3 us
    pallas_call x1, Pallas kernels, pairs(): pl.pallas_call(pairs_body, out_shape=(jax.ShapeDtypeStruct(pts.shape, jnp...  54.9 us
    pallas_call x1, Pallas kernels, reduce_scatter(): pl.pallas_call(scatter_body, out_shape=jax.ShapeDtypeStruct((3, clusters,...  37.4 us
    pallas_call x1, Pallas kernels, own_table(): pl.pallas_call(coeff_body, grid=(clusters // GROUP,), out_shape=jax.Shape...  8.09 us

profile of v5, /device:TPU:0, one launch (start us, length us, event | category | flops | bytes accessed | tf_op | source)
XLA Modules:
  0.0 163.7 jit_solution(11898364525554999380)
XLA Ops:
  0.6 0.7 fusion
  1.3 8.1 %coefficients.1.own_ref = f32[3,16,8,128]{3,2,1,0:T(8,128)} custom-call(f32[3,16,512]{2,1,0:T(8,128)} %bitcast.87, f32[3,16,512]{2,1,0:T(8,128)} %bitcast.88, f32[16,512,512]{2,1,0:T(8,128)} %inverse_ref.1), custom_call_target="tpu_custom_call" | custom-call | tf_op jit(solution)/shard_map/coefficients/pallas_call | solution.py:342
  9.4 0.0 copy-start
  9.4 0.9 copy-done
  10.4 0.0 copy-start.1
  10.4 0.0 copy-start.2
  10.4 0.0 copy-start.3
  10.4 60.3 %torus_gather.1 = f32[3,4,4,4,2,16,8,128]{7,6,5,4,3,2,1,0:T(8,128)S(1)} custom-call(f32[3,16,8,128]{3,2,1,0:T(8,128)S(1)} %copy-done), custom_call_target="tpu_custom_call" | custom-call | tf_op jit(solution)/shard_map/torus_gather/pallas_call | solution.py:159
  70.7 0.0 copy-done.1
  70.7 0.0 copy-done.2
  70.7 0.0 copy-done.3
  70.7 54.9 %pairs.1 = (f32[3,32,256]{2,1,0:T(8,128)}, f32[3,2048,512]{2,1,0:T(8,128)S(1)}) custom-call(s32[3,8,32]{2,1,0:T(8,128)S(1)} %pad_add_fusion.flat, f32[3,32,256]{2,1,0:T(8,128)S(1)} %bitcast.85, f32[3,32,256]{2,1,0:T(8,128)S(1)} %bitcast.86, s32[32,8,256]{2,1,0:T(8,128)S(1)} %copy-done.1, f32[3,16384,128]{2,1,0:T(8,128)S(1)} %bitcast.82), custom_call_target="tpu_custom_call" | custom-call | tf_op jit(solution)/shard_map/pairs/pallas_call | solution.py:516
  125.6 37.4 %torus_scatter.1 = f32[3,16,512]{2,1,0:T(8,128)S(1)} custom-call(f32[3,4,4,4,2,16,512]{6,5,4,3,2,1,0:T(8,128)S(1)} %bitcast.83), custom_call_target="tpu_custom_call" | custom-call | tf_op jit(solution)/shard_map/torus_scatter/pallas_call | solution.py:294
  163.0 0.6 copy.10
  (1 shorter events, 0.0 us)
Async XLA Ops:
  9.4 0.9 copy-start
  10.4 60.4 %copy-start.1 = (s32[32,8,256]{2,1,0:T(8,128)S(1)}, s32[32,8,256]{2,1,0:T(8,128)}, u32[]{:S(2)}) copy-start(s32[32,8,256]{2,1,0:T(8,128)} %lev_ref.1) | copy-start | bytes 786436
  10.4 60.4 %copy-start.2 = (f32[32,3,256]{2,0,1:T(8,128)S(1)}, f32[32,3,256]{2,0,1:T(8,128)}, u32[]{:S(2)}) copy-start(f32[32,3,256]{2,0,1:T(8,128)} %param.7) | copy-start | bytes 294916
  10.4 60.4 %copy-start.3 = (f32[32,3,256]{2,0,1:T(8,128)S(1)}, f32[32,3,256]{2,0,1:T(8,128)}, u32[]{:S(2)}) copy-start(f32[32,3,256]{2,0,1:T(8,128)} %param.8) | copy-start | bytes 294916
